TPU v7x, 32 devices: a whole 2x2x4 slice. The times are simulated.
32 devices in a mesh: dp: 2 (over x), fsdp: 4 (over z), ep: 4 (over y, core).
Axes of the slice: x: 2, y: 2, z: 4, core: 2. Of those that a mesh axis runs over, the one named last changes fastest.
Arguments:
- hidden: bfloat16 [65536, 4096], P(('dp', 'fsdp', 'ep')), parts along dimension 0
- norm_gain: bfloat16 [4096], replicated
- w_router: bfloat16 [4096, 16], replicated
- w_gate: bfloat16 [16, 4096, 688], P('ep', 'fsdp')
- w_up: bfloat16 [16, 4096, 688], P('ep', 'fsdp')
- w_down: bfloat16 [16, 688, 4096], P('ep', None, 'fsdp')
- top2_ids: int32 [65536, 2], P(('dp', 'fsdp', 'ep')), parts along dimension 0
Outputs:
- output: bfloat16 [65536, 4096], P(('dp', 'fsdp', 'ep')), parts along dimension 0
There are 2 independent parts. A program takes and returns all parts, laid end to end along the dimension named above; an argument that names none is the same for every part.
All inputs are finite; a program needn't handle non-finite values.
Results may differ from a plain program's by a relative error of at most 0.001.
Values are sent between devices in bfloat16 or wider.
A program may use at most 1 GiB of HBM per device.

v0:
```python
import jax
import jax.numpy as jnp
from jax import lax
from jax.sharding import PartitionSpec as P

EPS = 1e-5


def norm_and_gates(hidden, norm_gain, w_router, top2_ids):
    hidden_f32 = hidden.astype(jnp.float32)
    mean_sq = jnp.mean(hidden_f32 * hidden_f32, axis=-1, keepdims=True)
    normed = (hidden_f32 * lax.rsqrt(mean_sq + EPS) * norm_gain.astype(jnp.float32)).astype(jnp.bfloat16)
    logits = jnp.dot(normed, w_router, preferred_element_type=jnp.float32)
    gate_probs = jax.nn.softmax(jnp.take_along_axis(logits, top2_ids, axis=1), axis=-1)
    return hidden_f32, normed, gate_probs


def route_slots(top2_ids, num_experts, capacity):
    flat_ids = top2_ids.reshape(-1)
    onehot = (flat_ids[:, None] == jnp.arange(num_experts, dtype=jnp.int32)[None, :]).astype(jnp.int32)
    position = jnp.sum((jnp.cumsum(onehot, axis=0) - 1) * onehot, axis=1)
    slot_ids = jnp.where(position < capacity, flat_ids * capacity + position, num_experts * capacity)
    return slot_ids.reshape(top2_ids.shape)


def gather_rows(normed, slot_ids, num_slots):
    tok_count = slot_ids.shape[0]
    token_index = jnp.broadcast_to(jnp.arange(tok_count, dtype=jnp.int32)[:, None], slot_ids.shape)
    source = jnp.full((num_slots,), tok_count, dtype=jnp.int32).at[slot_ids.reshape(-1)].set(token_index.reshape(-1), mode='drop')
    return jnp.take(normed, source, axis=0, mode='fill', fill_value=0)


def take_slots(expert_rows, slot_ids):
    return jnp.take(expert_rows, slot_ids, axis=0, mode='fill', fill_value=0)


def expert_block(rows_in, gate_full, up_full, down_full):
    act_a = jnp.einsum('ecd,edf->ecf', rows_in, gate_full, preferred_element_type=jnp.float32)
    act_b = jnp.einsum('ecd,edf->ecf', rows_in, up_full, preferred_element_type=jnp.float32)
    hidden_act = (jax.nn.silu(act_a) * act_b).astype(jnp.bfloat16)
    return jnp.einsum('ecf,efd->ecd', hidden_act, down_full, preferred_element_type=jnp.float32).astype(jnp.bfloat16)


def local_block(hidden, norm_gain, w_router, w_gate, w_up, w_down, top2_ids):
    tok_local, d_model = hidden.shape
    num_experts = w_router.shape[1]
    capacity = (5 * tok_local + 2 * num_experts - 1) // (2 * num_experts)
    hidden_f32, normed, gate_probs = norm_and_gates(hidden, norm_gain, w_router, top2_ids)
    slot_ids = route_slots(top2_ids, num_experts, capacity)
    send_rows = gather_rows(normed, slot_ids, num_experts * capacity).reshape(num_experts, capacity, d_model)
    gate_full = lax.all_gather(w_gate, 'fsdp', axis=1, tiled=True)
    up_full = lax.all_gather(w_up, 'fsdp', axis=1, tiled=True)
    down_full = lax.all_gather(w_down, 'fsdp', axis=2, tiled=True)
    recv_rows = lax.all_to_all(send_rows, 'ep', 0, 1, tiled=True)
    expert_out = expert_block(recv_rows, gate_full, up_full, down_full)
    back_rows = lax.all_to_all(expert_out, 'ep', 1, 0, tiled=True)
    returned = take_slots(back_rows.reshape(num_experts * capacity, d_model), slot_ids)
    moe_sum = jnp.sum(gate_probs[:, :, None] * returned.astype(jnp.float32), axis=1)
    return (hidden_f32 + moe_sum).astype(jnp.bfloat16)


def solution(mesh):
    tok_spec = P(('dp', 'fsdp', 'ep'), None)
    in_specs = (tok_spec, P(None), P(None, None), P('ep', 'fsdp', None), P('ep', 'fsdp', None), P('ep', None, 'fsdp'), tok_spec)
    return jax.shard_map(local_block, mesh=mesh, in_specs=in_specs, out_specs=tok_spec, check_vma=False)
```

profile of v0, /device:TPU:1, one launch (start us, length us, event | category | flops | bytes accessed | tf_op | source)
XLA Modules:
  0.0 2116.6 jit_solution(916093222439412971)
XLA Ops:
  6.5 0.7 all-gather.4.cloned.1.call-update
  8.0 1.1 copy.35
  10.1 4.6 reduce-window.6
  15.3 0.7 broadcast_multiply_fusion
  17.6 0.7 convert_element_type.27
  19.2 15.5 scatter_custom_fusion
  34.9 7.5 fusion
  42.5 3.1 copy-done.2
  45.6 8.6 fusion.2
  54.2 77.3 %gather_fusion = bf16[5120,4096]{1,0:T(8,128)(2,1)} fusion(bf16[2048,4096]{1,0:T(8,128)(2,1)} %fusion.2, s32[5120]{0:T(1024)S(1)} %fusion.7), kind=kCustom, calls=%fused_computation | custom fusion | bytes 83906560 | tf_op jit(solution)/shard_map/jit(_take)/gather | solution.py:30
  131.5 28.2 %broadcast_select_fusion.1 = bf16[16,320,4096]{2,1,0:T(8,128)(2,1)} fusion(bf16[16,320,4096]{2,1,0:T(8,128)(2,1)} %bitcast.38, pred[16,320]{1,0:T(8,128)(4,1)S(1)} %broadcast_in_dim.58), kind=kLoop, calls=%fused_computation.10 | loop fusion | flops 20971520 | bytes 83891200 | tf_op jit(solution)/shard_map/jit(_take)/select_n | solution.py:30
  159.7 11.1 all-to-all-start
  171.5 451.2 %all-to-all-done = bf16[16,320,4096]{2,1,0:T(8,128)(2,1)} async-done(((bf16[16,320,4096]{2,1,0:T(8,128)(2,1)}), bf16[16,320,4096]{2,1,0:T(8,128)(2,1)}, u32[]{:S(2)}, u32[]{:S(2)}) %all-to-all-start) | async-done | bytes 41943072 | tf_op jit(solution)/shard_map/all_to_all | solution.py:54
  622.7 28.1 %copy.41 = bf16[4,4,320,4096]{3,2,1,0:T(8,128)(2,1)} copy(bf16[4,4,320,4096]{3,2,0,1:T(8,128)(2,1)} %bitcast.6) | data formatting | bytes 83886080 | tf_op jit(solution)/shard_map/all_to_all | solution.py:54
  650.8 42.1 %fusion.14 = f32[4,1280,688]{1,2,0:T(8,128)} fusion(bf16[4,1280,4096]{2,1,0:T(8,128)(2,1)} %bitcast.39, bf16[4,4096,688]{1,2,0:T(8,128)(2,1)} %all-gather.4.cloned.1.call-done), kind=kOutput, calls=%fused_computation.45 | convolution fusion | flops 28856811520 | bytes 78577664 | tf_op jit(solution)/shard_map/ecd,edf->ecf/dot_general | solution.py:38
  692.9 84.7 %all-gather.6.cloned.1.call-done = bf16[4,4096,688]{1,2,0:T(8,128)(2,1)} async-done(((bf16[4,1024,688]{1,2,0:T(8,128)(2,1)}), bf16[4,4096,688]{1,2,0:T(8,128)(2,1)}) %all-gather.6.cloned.1.call-update) | async-done | bytes 22544400 | tf_op jit(solution)/shard_map/all_gather | solution.py:52
  777.7 43.9 %multiply_convert_fusion = bf16[4,1280,688]{1,2,0:T(8,128)(2,1)} fusion(f32[4,1280,688]{1,2,0:T(8,128)} %fusion.14, bf16[4,1280,4096]{2,1,0:T(8,128)(2,1)} %bitcast.40, bf16[4,4096,688]{1,2,0:T(8,128)(2,1)} %all-gather.6.cloned.1.call-done), kind=kOutput, calls=%fused_computation.15 | convolution fusion | flops 28877946880 | bytes 85622784 | tf_op jit(solution)/shard_map/ecd,edf->ecf/dot_general | solution.py:39
  821.6 339.5 %all-gather.8.cloned.1.call-done = bf16[4,688,4096]{2,1,0:T(8,128)(2,1)} async-done(((bf16[4,688,1024]{2,1,0:T(8,128)(2,1)}), bf16[4,688,4096]{2,1,0:T(8,128)(2,1)}) %all-gather.8.cloned.1.call-update) | async-done | bytes 22544400 | tf_op jit(solution)/shard_map/all_gather | solution.py:53
  1161.1 40.7 %convolution_convert_fusion = bf16[4,1280,4096]{2,1,0:T(8,128)(2,1)} fusion(bf16[4,1280,688]{1,2,0:T(8,128)(2,1)} %multiply_convert_fusion, bf16[4,688,4096]{2,1,0:T(8,128)(2,1)} %all-gather.8.cloned.1.call-done), kind=kOutput, calls=%fused_computation.6 | convolution fusion | flops 28877783040 | bytes 71532544 | tf_op jit(solution)/shard_map/ecf,efd->ecd/dot_general | solution.py:41
  1201.8 52.0 %copy.42 = bf16[4,1280,4096]{2,0,1:T(4,128)(2,1)} copy(bf16[4,1280,4096]{2,1,0:T(8,128)(2,1)} %convolution_convert_fusion) | data formatting | bytes 83886080 | tf_op jit(solution)/shard_map/convert_element_type | solution.py:41
  1253.9 12.3 all-to-all-start.1
  1266.3 1.0 reduce_sum.43
  1268.6 1.1 reshape.132
  1270.6 10.2 fusion.13
  1280.8 33.0 %gather_fusion.2 = f32[4096]{0:T(1024)S(1)} fusion(f32[2048,16]{0,1:T(8,128)S(1)} %fusion.13, s32[4096]{0:T(1024)S(1)} %reshape.138), kind=kCustom, calls=%fused_computation.2 | custom fusion | bytes 65536 | tf_op jit(solution)/shard_map/jit(take_along_axis)/gather | solution.py:14
  1313.8 1.0 reshape.141
  1316.2 401.6 %all-to-all-done.1 = bf16[4,1280,4096]{2,0,1:T(4,128)(2,1)} async-done(((bf16[4,1280,4096]{2,0,1:T(4,128)(2,1)}), bf16[4,1280,4096]{2,0,1:T(4,128)(2,1)}, u32[]{:S(2)}, u32[]{:S(2)}) %all-to-all-start.1) | async-done | bytes 41943072 | tf_op jit(solution)/shard_map/all_to_all | solution.py:56
  1717.8 36.1 %copy.43 = bf16[4,4,320,4096]{3,2,0,1:T(8,128)(2,1)} copy(bf16[4,4,320,4096]{3,0,2,1:T(4,128)(2,1)} %bitcast.8) | data formatting | bytes 83886080 | tf_op jit(solution)/shard_map/all_to_all | solution.py:56
  1753.8 154.1 %gather_fusion.1 = bf16[4096,4096]{1,0:T(8,128)(2,1)} fusion(bf16[5120,4096]{1,0:T(8,128)(2,1)} %bitcast.37, s32[4096]{0:T(1024)S(1)} %broadcast_clamp_fusion), kind=kCustom, calls=%fused_computation.1 | custom fusion | bytes 67125248 | tf_op jit(solution)/shard_map/jit(_take)/gather | solution.py:34
  1907.9 53.1 %reshape.131 = bf16[2048,2,4096]{2,1,0:T(2,128)(2,1)} reshape(bf16[4096,4096]{1,0:T(8,128)(2,1)} %gather_fusion.1) | data formatting | bytes 67108864 | tf_op jit(solution)/shard_map/jit(_take)/gather | solution.py:34
  1961.0 126.7 %multiply_reduce_fusion = f32[2048,4096]{1,0:T(8,128)} fusion(bf16[2048,2,4096]{2,1,0:T(2,128)(2,1)} %reshape.131, pred[2048,2]{1,0:T(8,128)(4,1)S(1)} %copy.39, f32[2048,2]{1,0:T(8,128)S(1)} %copy.34), kind=kLoop, calls=%fused_computation.4 | loop fusion | flops 58720256 | bytes 67129344 | tf_op jit(solution)/shard_map/reduce_sum | solution.py:58
  2087.7 22.0 %fusion.3 = bf16[2048,4096]{1,0:T(8,128)(2,1)} fusion(f32[2048,4096]{1,0:T(8,128)} %multiply_reduce_fusion, bf16[2048,4096]{1,0:T(8,128)(2,1)} %param.7), kind=kLoop, calls=%fused_computation.14 | loop fusion | flops 25165824 | bytes 67108864 | tf_op jit(solution)/shard_map/convert_element_type | solution.py:59
  (52 shorter events, 9.1 us)
Async XLA Ops:
  6.5 1264.0 %copy-start = (bf16[4096,16]{0,1:T(8,128)(2,1)S(1)}, bf16[4096,16]{0,1:T(8,128)(2,1)}, u32[]{:S(2)}) copy-start(bf16[4096,16]{0,1:T(8,128)(2,1)} %param.9) | copy-start | bytes 393220
  6.5 644.3 %all-gather.4.cloned.1.call-start = ((), (), s32[]{:S(2)}) async-start(), calls=%async_computation.2 | async-start | bytes 28180480 | tf_op jit(solution)/shard_map/all_gather | solution.py:51
  7.3 770.4 %all-gather.6.cloned.1.call-start = ((), (), s32[]{:S(2)}) async-start(), calls=%async_computation.3 | async-start | bytes 28180480 | tf_op jit(solution)/shard_map/all_gather | solution.py:52
  18.6 0.6 copy-start.5
  34.9 10.7 copy-start.2
  159.7 463.0 %all-to-all-start = ((bf16[16,320,4096]{2,1,0:T(8,128)(2,1)}), bf16[16,320,4096]{2,1,0:T(8,128)(2,1)}, u32[]{:S(2)}, u32[]{:S(2)}) async-start(bf16[16,320,4096]{2,1,0:T(8,128)(2,1)} %broadcast_select_fusion.1), calls=%async_computation | async-start | bytes 83886080 | tf_op jit(solution)/shard_map/all_to_all | solution.py:54
  170.8 990.3 %all-gather.8.cloned.1.call-start = ((), (), s32[]{:S(2)}) async-start(), calls=%async_computation.4 | async-start | bytes 28180480 | tf_op jit(solution)/shard_map/all_gather | solution.py:53
  1253.9 12.4 copy-start.6
  1253.9 13.7 copy-start.3
  1253.9 463.9 %all-to-all-start.1 = ((bf16[4,1280,4096]{2,0,1:T(4,128)(2,1)}), bf16[4,1280,4096]{2,0,1:T(4,128)(2,1)}, u32[]{:S(2)}, u32[]{:S(2)}) async-start(bf16[4,1280,4096]{2,0,1:T(4,128)(2,1)} %copy.42), calls=%async_computation.1 | async-start | bytes 83886080 | tf_op jit(solution)/shard_map/all_to_all | solution.py:56
  1280.8 34.4 %copy-start.4 = (s32[2048,2]{0,1:T(2,128)S(1)}, s32[2048,2]{0,1:T(2,128)}, u32[]{:S(2)}) copy-start(s32[2048,2]{0,1:T(2,128)} %param.13) | copy-start | bytes 49156
  1280.8 34.9 %copy-start.8 = (pred[2048,2]{0,1:T(4,128)(4,1)S(1)}, pred[2048,2]{0,1:T(4,128)(4,1)}, u32[]{:S(2)}) copy-start(pred[2048,2]{0,1:T(4,128)(4,1)} %get-tuple-element.7) | copy-start | bytes 12292
  1280.8 35.4 %copy-start.7 = (s32[4096]{0:T(1024)S(1)}, s32[4096]{0:T(1024)}, u32[]{:S(2)}) copy-start(s32[4096]{0:T(1024)} %reshape.132) | copy-start | bytes 49156
  1961.0 148.6 %copy-start.1 = (bf16[4096,16]{0,1:T(8,128)(2,1)S(1)}, bf16[4096,16]{0,1:T(8,128)(2,1)}, u32[]{:S(2)}) copy-start(bf16[4096,16]{0,1:T(8,128)(2,1)} %param.9) | copy-start | bytes 393220
Sparse Core Ops, SparseCore 0:
  8.9 385.2 all-gather.3
  395.8 381.8 all-gather.5
  779.2 381.8 all-gather.7
where the time goes:
time: 2130 us; the launch traced here: 2120 us
  waiting for transfers between devices  1280 us (60%)
  local copies, waits for them, and re-layouts  463 us (22%)
  other arithmetic  200 us (9%)
  matrix products  137 us (6%)
  starting transfers between devices  24 us (1%)
    all_to_all x1, waiting for transfers between devices, local_block(): recv_rows = lax.all_to_all(send_rows, 'ep', 0, 1, tiled=True)  451 us
    all_to_all x1, waiting for transfers between devices, local_block(): back_rows = lax.all_to_all(expert_out, 'ep', 1, 0, tiled=True)  402 us
    all_gather x1, waiting for transfers between devices, local_block(): down_full = lax.all_gather(w_down, 'fsdp', axis=2, tiled=True)  340 us
    gather x2, local copies, waits for them, and re-layouts, take_slots(): return jnp.take(expert_rows, slot_ids, axis=0, mode='fill', fill_value=0)  207 us
    reduce_sum x1, other arithmetic, local_block(): jnp.sum(gate_probs[:, :, None] * returned.astype(jnp.float32), axis=1)  127 us
    all_gather x1, waiting for transfers between devices, local_block(): up_full = lax.all_gather(w_up, 'fsdp', axis=1, tiled=True)  84.7 us
    gather x1, local copies, waits for them, and re-layouts, gather_rows(): return jnp.take(normed, source, axis=0, mode='fill', fill_value=0)  77.3 us
    convert_element_type x1, local copies, waits for them, and re-layouts, expert_block(): jnp.einsum('ecf,efd->ecd', hidden_act, down_full, preferred_element_type=...  52 us
  transfers between devices with their start and end apart: 5, of which 4 were waited for; matrix products, arithmetic and copies ran while one was open for 15% of the time, Pallas kernels for 0%

commit v1 on v0

v1 whole, which is shorter than its diff:
```python
import functools

import jax
import jax.numpy as jnp
from jax import lax
from jax.experimental import pallas as pl
from jax.experimental.pallas import tpu as pltpu
from jax.sharding import PartitionSpec as P

EPS = 1e-5
MESH = pl.DeviceIdType.MESH
HBM = pl.BlockSpec(memory_space=pl.ANY)
VMEM = pl.BlockSpec(memory_space=pltpu.VMEM)
F = 4
E = 4
CHUNKS = 8


def exchange_kernel(hid, *refs):
    (wg, wu, wd, hall, gf, uf, df, own_sem, hy_s, hy_r, hs_s, hs_r, hf_s, hf_r,
     zr_s, zl_s, z_r, x_s, x_r) = refs
    half, z, j = lax.axis_index('dp'), lax.axis_index('fsdp'), lax.axis_index('ep')
    sib = j + 1 - 2 * (j % 2)
    across = (j + 2) % E
    experts, _, width = wg.shape
    part = width // 2
    rows = hid.shape[0] // CHUNKS
    pieces = [(src, dst, e) for e in range(experts) for src, dst in ((wg, gf), (wu, uf), (wd, df))]

    def region(p, f, h):
        return pieces[p][1].at[pieces[p][2], :, pl.ds(pl.multiple_of(f * width + h * part, 128), part)]

    def own(p):
        return pieces[p][0].at[pieces[p][2], :, pl.ds(pl.multiple_of(half * part, 128), part)]

    def along_z(p, f, src, step, sems):
        return pltpu.make_async_remote_copy(
            src_ref=src, dst_ref=region(p, f, half), send_sem=sems.at[p, f], recv_sem=z_r.at[p, f],
            device_id={'fsdp': z + step}, device_id_type=MESH)

    def along_x(p, f, h):
        return pltpu.make_async_remote_copy(
            src_ref=region(p, f, h), dst_ref=region(p, f, h), send_sem=x_s.at[p, f], recv_sem=x_r.at[p, f],
            device_id={'dp': 1 - half}, device_id_type=MESH)

    def tokens(src, owner, c, send, recv, target):
        return pltpu.make_async_remote_copy(
            src_ref=src, dst_ref=hall.at[owner, pl.ds(c * rows, rows)], send_sem=send.at[c], recv_sem=recv.at[c],
            device_id={'ep': target}, device_id_type=MESH)

    def mine(c):
        return hid.at[pl.ds(c * rows, rows)]

    def local(c):
        return pltpu.make_async_copy(mine(c), hall.at[j, pl.ds(c * rows, rows)], own_sem.at[c])

    for p in range(len(pieces)):
        pl.when(z < F - 1)(lambda p=p: along_z(p, z, own(p), 1, zr_s).start())
        pl.when(z > 0)(lambda p=p: along_z(p, z, own(p), -1, zl_s).start())
    for c in range(CHUNKS):
        tokens(mine(c), j, c, hy_s, hy_r, across).start()
    for c in range(CHUNKS):
        tokens(mine(c), j, c, hs_s, hs_r, sib).start()
        local(c).start()

    def arrive(p, d):
        def from_left():
            f = z - d
            along_z(p, f, own(p), 1, zr_s).wait_recv()
            pl.when(z < F - 1)(lambda: along_z(p, f, region(p, f, half), 1, zr_s).start())
            along_x(p, f, half).start()

        def from_right():
            f = z + d
            along_z(p, f, own(p), 1, zr_s).wait_recv()
            pl.when(z > 0)(lambda: along_z(p, f, region(p, f, half), -1, zl_s).start())
            along_x(p, f, half).start()

        pl.when(z >= d)(from_left)
        pl.when(z < F - d)(from_right)

    total = (F - 1) * len(pieces)
    done = 0
    for i, (d, p) in enumerate((d, p) for d in range(1, F) for p in range(len(pieces))):
        arrive(p, d)
        while done < CHUNKS and (done + 1) * total * 3 <= (i + 1) * CHUNKS * 4:
            tokens(mine(done), across, done, hy_s, hy_r, across).wait_recv()
            tokens(hall.at[across, pl.ds(done * rows, rows)], across, done, hf_s, hf_r, sib).start()
            done += 1
    for c in range(CHUNKS):
        tokens(mine(c), j, c, hy_s, hy_r, across).wait_send()
        tokens(mine(c), j, c, hs_s, hs_r, sib).wait()
        tokens(mine(c), j, c, hf_s, hf_r, sib).wait()
        local(c).wait()
    for p in range(len(pieces)):
        for f in range(F):
            def to_right(p=p, f=f):
                along_z(p, f, own(p), 1, zr_s).wait_send()

            def to_left(p=p, f=f):
                along_z(p, f, own(p), -1, zl_s).wait_send()

            def both(p=p, f=f):
                along_x(p, f, half).wait_send()
                along_x(p, f, 1 - half).wait_recv()

            pl.when(jnp.logical_and(z < F - 1, f <= z))(to_right)
            pl.when(jnp.logical_and(z > 0, f >= z))(to_left)
            pl.when(z != f)(both)


def exchange(hidden, w_gate, w_up, w_down):
    experts, ff, width = w_gate.shape
    full = jax.ShapeDtypeStruct((experts, ff, F * width), w_gate.dtype)
    dma = pltpu.SemaphoreType.DMA
    grid_sems = [dma((3 * experts, F)) for _ in range(5)]
    return pl.pallas_call(
        exchange_kernel,
        out_shape=(jax.ShapeDtypeStruct((E,) + hidden.shape, hidden.dtype), full, full, full),
        in_specs=[HBM] * 4,
        out_specs=(HBM,) * 4,
        scratch_shapes=[dma((CHUNKS,)) for _ in range(7)] + grid_sems,
        compiler_params=pltpu.CompilerParams(has_side_effects=True),
        name='exchange',
    )(hidden, w_gate, w_up, w_down)


O_SLOTS = 4


def expert_kernel(rows_in, gain, wg, wu, wd, gf, uf, df, back, wbuf, xbuf, obuf, hbuf, acc_a, acc_b,
                  w_sem, x_sem, o_sem, r_sem):
    z, j = lax.axis_index('fsdp'), lax.axis_index('ep')
    y, core = j // 2, j % 2
    experts, _, capacity, d_model = rows_in.shape
    width = wg.shape[2]
    blocks = experts * E
    sources = ((wg, gf), (wu, uf), (wd, df))

    def owner(q):
        return ((y + 1 - q // 2) % 2) * 2 + (core + q % 2) % 2

    def weights(e, act):
        slot = e % 2
        for t, (part, whole) in enumerate(sources):
            for f in range(F):
                cols = pl.ds(f * width, width)
                dst, sem = wbuf.at[slot, t, :, cols], w_sem.at[slot, t * F + f]
                pl.when(z == f)(lambda: act(pltpu.make_async_copy(part.at[e], dst, sem)))
                pl.when(z != f)(lambda: act(pltpu.make_async_copy(whole.at[e, :, cols], dst, sem)))

    def x_load(i):
        return pltpu.make_async_copy(rows_in.at[i // E, owner(i % E)], xbuf.at[i % 2], x_sem.at[i % 2])

    def send(i):
        return pltpu.make_async_remote_copy(
            src_ref=obuf.at[i % O_SLOTS], dst_ref=back.at[j * experts + i // E], send_sem=o_sem.at[i % O_SLOTS],
            recv_sem=r_sem.at[j * experts + i // E], device_id={'ep': owner(i % E)}, device_id_type=MESH)

    def keep(i):
        return pltpu.make_async_copy(obuf.at[i % O_SLOTS], back.at[j * experts + i // E], o_sem.at[i % O_SLOTS])

    def sent(i):
        pl.when(i % E == 2)(lambda: keep(i).wait())
        pl.when(i % E != 2)(lambda: send(i).wait_send())

    weights(0, lambda copy: copy.start())
    x_load(0).start()

    def block(i, carry):
        e = i // E
        slot, xs, os = e % 2, i % 2, i % O_SLOTS

        @pl.when(i % E == 0)
        def _():
            weights(e, lambda copy: copy.wait())
            pl.when(e + 1 < experts)(lambda: weights(e + 1, lambda copy: copy.start()))

        x_load(i).wait()
        pl.when(i + 1 < blocks)(lambda: x_load(i + 1).start())

        step = 16 if capacity % 16 == 0 else capacity
        def norm(r, c):
            rs = pl.ds(pl.multiple_of(r * step, step), step)
            x = xbuf[xs, rs, :].astype(jnp.float32)
            scale = lax.rsqrt(jnp.mean(x * x, axis=-1, keepdims=True) + EPS)
            xbuf[xs, rs, :] = (x * scale * gain[...]).astype(jnp.bfloat16)
            return c
        lax.fori_loop(0, capacity // step, norm, 0)

        acc_a[...] = jnp.zeros_like(acc_a)
        acc_b[...] = jnp.zeros_like(acc_b)
        def first(k, c):
            ks = pl.ds(pl.multiple_of(k * width, 128), width)
            u = xbuf[xs, :, ks]
            dims = (((1,), (1,)), ((), ()))
            acc_a[...] += lax.dot_general(u, wbuf[slot, 0, :, ks], dims, preferred_element_type=jnp.float32)
            acc_b[...] += lax.dot_general(u, wbuf[slot, 1, :, ks], dims, preferred_element_type=jnp.float32)
            return c
        lax.fori_loop(0, F, first, 0)
        a = acc_a[...]
        hbuf[...] = (a * jax.nn.sigmoid(a) * acc_b[...]).astype(jnp.bfloat16)

        pl.when(i >= O_SLOTS)(lambda: sent(i - O_SLOTS))
        def second(n, c):
            ns = pl.ds(pl.multiple_of(n * width, 128), width)
            obuf[os, :, ns] = jnp.dot(
                hbuf[...], wbuf[slot, 2, :, ns], preferred_element_type=jnp.float32).astype(jnp.bfloat16)
            return c
        lax.fori_loop(0, F, second, 0)
        pl.when(i % E == 2)(lambda: keep(i).start())
        pl.when(i % E != 2)(lambda: send(i).start())
        return carry

    lax.fori_loop(0, blocks, block, 0)
    for i in range(blocks - O_SLOTS, blocks):
        sent(i)

    def arrived(n, c):
        def wait():
            pltpu.make_async_remote_copy(
                src_ref=obuf.at[0], dst_ref=back.at[n], send_sem=o_sem.at[0], recv_sem=r_sem.at[n],
                device_id={'ep': n // experts}, device_id_type=MESH).wait_recv()
        pl.when(n // experts != j)(wait)
        return c
    lax.fori_loop(0, blocks, arrived, 0)


def run_experts(rows_in, gain, w_gate, w_up, w_down, gate_full, up_full, down_full):
    experts, _, capacity, d_model = rows_in.shape
    ff = w_gate.shape[1]
    dma = pltpu.SemaphoreType.DMA
    return pl.pallas_call(
        expert_kernel,
        out_shape=jax.ShapeDtypeStruct((E * experts, capacity, d_model), jnp.bfloat16),
        in_specs=[HBM, VMEM] + [HBM] * 6,
        out_specs=HBM,
        scratch_shapes=[
            pltpu.VMEM((2, 3, ff, d_model), jnp.bfloat16),
            pltpu.VMEM((2, capacity, d_model), jnp.bfloat16),
            pltpu.VMEM((O_SLOTS, capacity, d_model), jnp.bfloat16),
            pltpu.VMEM((capacity, ff), jnp.bfloat16),
            pltpu.VMEM((capacity, ff), jnp.float32),
            pltpu.VMEM((capacity, ff), jnp.float32),
            dma((2, 3 * F)), dma((2,)), dma((O_SLOTS,)), dma((E * experts,)),
        ],
        compiler_params=pltpu.CompilerParams(has_side_effects=True, vmem_limit_bytes=62 * 1024 * 1024),
        name='experts',
    )(rows_in, gain, w_gate, w_up, w_down, gate_full, up_full, down_full)


def gate_values(hidden_f32, norm_gain, w_router, top2_ids):
    mean_sq = jnp.mean(hidden_f32 * hidden_f32, axis=-1, keepdims=True)
    normed = (hidden_f32 * lax.rsqrt(mean_sq + EPS) * norm_gain.astype(jnp.float32)).astype(jnp.bfloat16)
    logits = jnp.dot(normed, w_router, preferred_element_type=jnp.float32)
    experts = jnp.arange(w_router.shape[1], dtype=jnp.int32)
    picked = [jnp.sum(jnp.where(top2_ids[:, k:k + 1] == experts, logits, 0.0), axis=1) for k in range(2)]
    return jax.nn.softmax(jnp.stack(picked, axis=1), axis=-1)


def local_block(hidden, norm_gain, w_router, w_gate, w_up, w_down, top2_ids):
    tok_local, d_model = hidden.shape
    num_experts = w_router.shape[1]
    capacity = (5 * tok_local + 2 * num_experts - 1) // (2 * num_experts)
    experts = num_experts // E
    gate_t, up_t = jnp.swapaxes(w_gate, 1, 2), jnp.swapaxes(w_up, 1, 2)

    flat_ids = top2_ids.reshape(-1)
    onehot = (flat_ids[:, None] == jnp.arange(num_experts, dtype=jnp.int32)[None, :]).astype(jnp.int32)
    position = jnp.sum((jnp.cumsum(onehot, axis=0) - 1) * onehot, axis=1)
    keep = (position < capacity).reshape(top2_ids.shape)
    slot_ids = jnp.where(position < capacity, flat_ids * capacity + position, num_experts * capacity)
    token_index = jnp.arange(2 * tok_local, dtype=jnp.int32) // 2
    source = jnp.zeros((num_experts * capacity,), jnp.int32).at[slot_ids].set(token_index, mode='drop')
    source = lax.all_to_all(source.reshape(E, experts * capacity), 'ep', 0, 0)
    source = source.reshape(E, experts, capacity) + (jnp.arange(E, dtype=jnp.int32) * tok_local)[:, None, None]
    source = jnp.swapaxes(source, 0, 1).reshape(-1)

    everyone, gate_full, up_full, down_full = exchange(hidden, gate_t, up_t, w_down)
    rows_in = jnp.take(everyone.reshape(E * tok_local, d_model), source, axis=0, mode='clip')
    rows_in = rows_in.reshape(experts, E, capacity, d_model)
    gain = norm_gain.astype(jnp.float32).reshape(1, d_model)
    back = run_experts(rows_in, gain, gate_t, up_t, w_down, gate_full, up_full, down_full)
    back = back.reshape(num_experts * capacity, d_model)

    hidden_f32 = hidden.astype(jnp.float32)
    gate_probs = gate_values(hidden_f32, norm_gain, w_router, top2_ids)
    slot_ids = slot_ids.reshape(top2_ids.shape)
    moe = [
        jnp.where(keep[:, k:k + 1],
                  gate_probs[:, k:k + 1] * jnp.take(back, slot_ids[:, k], axis=0, mode='clip').astype(jnp.float32), 0.0)
        for k in range(2)
    ]
    return (hidden_f32 + (moe[0] + moe[1])).astype(jnp.bfloat16)


def solution(mesh):
    tok_spec = P(('dp', 'fsdp', 'ep'), None)
    in_specs = (tok_spec, P(None), P(None, None), P('ep', 'fsdp', None), P('ep', 'fsdp', None), P('ep', None, 'fsdp'), tok_spec)
    return jax.shard_map(local_block, mesh=mesh, in_specs=in_specs, out_specs=tok_spec, check_vma=False)
```

time: 2130 us -> 1510 us (0.71)
  waiting for transfers between devices: 1280 us -> 0.01 us
  Pallas kernels: 0 us -> 1050 us
  other arithmetic: 200 us -> 43.7 us
  matrix products: 137 us -> 8.19 us
  local copies, waits for them, and re-layouts: 463 us -> 399 us
    pallas_call x0 -> x2, Pallas kernels: none -> 1050 us  [the longest x1 571 us: exchange(): pl.pallas_call(exchange_kernel, out_shape=(jax.ShapeDtypeStruct((E,) + hi...]
    all_to_all x2 -> x1, waiting for transfers between devices: 853 us -> 0.01 us  [local_block(): source = lax.all_to_all(source.reshape(E, experts * capacity), 'ep', 0, 0)]
    all_gather x3 -> x0, waiting for transfers between devices: 424 us -> none  [the longest x1 340 us: local_block(): down_full = lax.all_gather(w_down, 'fsdp', axis=2, tiled=True)]
    dot_general x4 -> x1, matrix products: 137 us -> 8.19 us  [gate_values(): logits = jnp.dot(normed, w_router, preferred_element_type=jnp.float32)]
    reduce_sum x4 -> x3, other arithmetic: 134 us -> 7.43 us  [the longest x1 7.21 us: gate_values(): mean_sq = jnp.mean(hidden_f32 * hidden_f32, axis=-1, keepdims=True)]
    all_to_all x2 -> x0, local copies, waits for them, and re-layouts: 64.1 us -> none  [the longest x1 36.1 us: local_block(): back_rows = lax.all_to_all(expert_out, 'ep', 1, 0, tiled=True)]
    gather x8 -> x3, local copies, waits for them, and re-layouts: 320 us -> 374 us  [the longest x1 231 us: local_block(): jnp.take(everyone.reshape(E * tok_local, d_model), source, axis=0, mode='...]
    convert_element_type x1 -> x0, local copies, waits for them, and re-layouts: 52 us -> none  [expert_block(): jnp.einsum('ecf,efd->ecd', hidden_act, down_full, preferred_element_type=...]
  transfers between devices with their start and end apart: 5 -> 1, of which waited for: 4 -> 0; matrix products, arithmetic and copies ran while one was open for 15% -> 1% of each run, Pallas kernels for 0% -> 38%
where the time goes in v1:
time: 1510 us
  Pallas kernels  1050 us (70%)
  local copies, waits for them, and re-layouts  399 us (26%)
  other arithmetic  43.7 us (3%)
    pallas_call x1, Pallas kernels, exchange(): pl.pallas_call(exchange_kernel, out_shape=(jax.ShapeDtypeStruct((E,) + hi...  571 us
    pallas_call x1, Pallas kernels, run_experts(): pl.pallas_call(expert_kernel, out_shape=jax.ShapeDtypeStruct((E * experts...  480 us
    gather x1, local copies, waits for them, and re-layouts, local_block(): jnp.take(everyone.reshape(E * tok_local, d_model), source, axis=0, mode='...  231 us
    gather x2, local copies, waits for them, and re-layouts, local_block(): jnp.take(back, slot_ids[:, k], axis=0, mode='clip').astype(jnp.float32)  143 us
  transfers between devices with their start and end apart: 1, of which 0 were waited for; matrix products, arithmetic and copies ran while one was open for 1% of the time, Pallas kernels for 38%

profile of v1, /device:TPU:1, one launch (start us, length us, event | category | flops | bytes accessed | tf_op | source)
XLA Modules:
  0.0 1506.7 jit_solution(2748427962139875058)
XLA Ops:
  0.0 1.1 copy.15
  1.1 0.5 eq.59
  1.6 0.5 eq.55
  2.1 4.6 reduce-window.6
  6.7 0.5 slice_reduce_fusion.4
  7.2 0.2 reduce-window.9
  7.4 0.1 add_add_fusion
  7.5 0.2 fusion.9
  7.7 1.0 reduce_sum.50
  8.7 1.1 add_select_fusion
  9.8 1.8 mul.72
  11.7 16.1 %scatter_custom_fusion = s32[5120]{0:T(1024)} fusion(s32[4096]{0:T(1024)S(1)} %bitcast.50, s32[4096]{0:T(1024)S(1)} %add_select_fusion.1, s32[]{:T(128)} %constant.16.clone.1), kind=kCustom, calls=%fused_computation.46 | custom fusion | bytes 20484 | tf_op jit(solution)/shard_map/scatter | solution.py:274
  27.8 4.3 all-to-all-start
  32.1 0.8 fusion.19
  32.9 0.1 broadcast_compare_fusion
  33.1 7.2 fusion
  40.3 0.7 convert_element_type.26
  41.0 8.2 select_reduce_fusion
  49.3 0.6 fusion.18
  49.9 1.5 slice_reduce_fusion.3
  51.4 0.9 slice_reduce_fusion.1
  52.3 0.6 broadcast_clamp_fusion.1
  53.0 571.3 %exchange.1 = (bf16[4,2048,4096]{2,1,0:T(8,128)(2,1)}, bf16[4,688,4096]{2,1,0:T(8,128)(2,1)}, bf16[4,688,4096]{2,1,0:T(8,128)(2,1)}, bf16[4,688,4096]{2,1,0:T(8,128)(2,1)}) custom-call(bf16[2048,4096]{1,0:T(8,128)(2,1)} %hid.1, bf16[4,688,1024]{2,1,0:T(8,128)(2,1)} %bitcast.36, bf16[4,688,1024]{2,1,0:T(8,128)(2,1)} %bitcast.38, bf16[4,688,1024]{2,1,0:T(8,128)(2,1)} %wd.1), custom_call_target="tpu_custom_call" | custom-call | tf_op jit(solution)/shard_map/exchange/pallas_call | solution.py:117
  624.3 0.1 reduce.4
  624.4 0.1 reshape.103
  624.4 0.1 add_bitcast_fusion
  624.5 0.1 reshape.108
  624.6 230.8 %gather_fusion = bf16[5120,4096]{1,0:T(8,128)(2,1)} fusion(bf16[8192,4096]{1,0:T(8,128)(2,1)} %bitcast.8, s32[5120]{0:T(1024)S(1)} %broadcast_clamp_fusion), kind=kCustom, calls=%fused_computation | custom fusion | bytes 83906560 | tf_op jit(solution)/shard_map/jit(_take)/gather | solution.py:280
  855.5 479.5 %experts.1 = bf16[16,320,4096]{2,1,0:T(8,128)(2,1)} custom-call(bf16[4,4,320,4096]{3,2,1,0:T(8,128)(2,1)} %bitcast.35, f32[1,4096]{1,0:T(1,128)} %bitcast.46, bf16[4,688,1024]{2,1,0:T(8,128)(2,1)} %bitcast.37, bf16[4,688,1024]{2,1,0:T(8,128)(2,1)} %bitcast.39, bf16[4,688,1024]{2,1,0:T(8,128)(2,1)} %wd.1, bf16[4,688,4096]{2,1,0:T(8,128)(2,1)} %get-tuple-element.10.gf, ...), custom_call_target="tpu_custom_call" | custom-call | tf_op jit(solution)/shard_map/experts/pallas_call | solution.py:233
  1335.0 69.0 %gather_fusion.2 = bf16[2048,4096]{1,0:T(8,128)(2,1)} fusion(bf16[5120,4096]{1,0:T(8,128)(2,1)} %bitcast.33, s32[2048]{0:T(1024)S(1)} %copy-done.6), kind=kCustom, calls=%fused_computation.2 | custom fusion | bytes 33562624 | tf_op jit(solution)/shard_map/jit(_take)/gather | solution.py:291
  1404.0 74.1 %gather_fusion.1 = bf16[2048,4096]{1,0:T(8,128)(2,1)} fusion(bf16[5120,4096]{1,0:T(8,128)(2,1)} %bitcast.34, s32[2048]{0:T(1024)S(1)} %copy-done.5), kind=kCustom, calls=%fused_computation.1 | custom fusion | bytes 33562624 | tf_op jit(solution)/shard_map/jit(_take)/gather | solution.py:291
  1478.1 28.5 %fusion.3 = bf16[2048,4096]{1,0:T(8,128)(2,1)} fusion(bf16[2048,4096]{1,0:T(8,128)(2,1)} %hid.1, bf16[2048,4096]{1,0:T(8,128)(2,1)} %gather_fusion.2, bf16[2048,4096]{1,0:T(8,128)(2,1)} %gather_fusion.1, f32[2048]{0:T(1024)S(1)} %bitcast.49, f32[2048]{0:T(1024)S(1)} %bitcast.48, pred[2048]{0:T(1024)(128)(4,1)S(1)} %copy-done.8, pred[2048]{0:T(1024)(128)(4,1)S(1)} %copy-done.7), kind=kLoop, calls=%fused_computation.10 | loop fusion | flops 83886080 | bytes 67129344 | tf_op jit(solution)/shard_map/convert_element_type | solution.py:294
  (29 shorter events, 0.2 us)
Async XLA Ops:
  0.0 41.0 %copy-start = (bf16[4096,16]{0,1:T(8,128)(2,1)S(1)}, bf16[4096,16]{0,1:T(8,128)(2,1)}, u32[]{:S(2)}) copy-start(bf16[4096,16]{0,1:T(8,128)(2,1)} %param.9) | copy-start | bytes 393220
  27.8 596.4 %all-to-all-start = ((s32[4,1,1280]{2,1,0:T(1,128)}), s32[4,1,1280]{2,1,0:T(1,128)S(1)}, u32[]{:S(2)}, u32[]{:S(2)}) async-start(s32[4,1,1280]{2,1,0:T(1,128)} %bitcast.11), calls=%async_computation | async-start | bytes 40960 | tf_op jit(solution)/shard_map/all_to_all | solution.py:275
  41.0 583.3 %copy-start.2 = (f32[4096]{0:T(1024)}, f32[4096]{0:T(1024)S(1)}, u32[]{:S(2)}) copy-start(f32[4096]{0:T(1024)S(1)} %convert_element_type.26) | copy-start | bytes 49156
  855.5 479.5 %copy-start.6 = (s32[2048]{0:T(1024)S(1)}, s32[2048]{0:T(1024)}, u32[]{:S(2)}) copy-start(s32[2048]{0:T(1024)} %get-tuple-element.25) | copy-start | bytes 24580
  1335.0 69.0 %copy-start.5 = (s32[2048]{0:T(1024)S(1)}, s32[2048]{0:T(1024)}, u32[]{:S(2)}) copy-start(s32[2048]{0:T(1024)} %get-tuple-element.26) | copy-start | bytes 24580
  1404.0 74.1 %copy-start.3 = (f32[2048,1]{0,1:T(1,128)S(1)}, f32[2048,1]{0,1:T(1,128)}, u32[]{:S(2)}) copy-start(f32[2048,1]{0,1:T(1,128)} %get-tuple-element.21) | copy-start | bytes 24580
  1404.0 74.1 %copy-start.4 = (f32[2048,1]{0,1:T(1,128)S(1)}, f32[2048,1]{0,1:T(1,128)}, u32[]{:S(2)}) copy-start(f32[2048,1]{0,1:T(1,128)} %get-tuple-element.22) | copy-start | bytes 24580
  1404.0 74.1 %copy-start.7 = (pred[2048]{0:T(1024)(128)(4,1)S(1)}, pred[2048]{0:T(1024)(128)(4,1)}, u32[]{:S(2)}) copy-start(pred[2048]{0:T(1024)(128)(4,1)} %get-tuple-element.15) | copy-start | bytes 6148
  1404.0 74.1 %copy-start.8 = (pred[2048]{0:T(1024)(128)(4,1)S(1)}, pred[2048]{0:T(1024)(128)(4,1)}, u32[]{:S(2)}) copy-start(pred[2048]{0:T(1024)(128)(4,1)} %get-tuple-element.16) | copy-start | bytes 6148
  1478.1 28.6 %copy-start.1 = (bf16[4096,16]{0,1:T(8,128)(2,1)S(1)}, bf16[4096,16]{0,1:T(8,128)(2,1)}, u32[]{:S(2)}) copy-start(bf16[4096,16]{0,1:T(8,128)(2,1)} %param.9) | copy-start | bytes 393220

commit v2 on v0

v2 whole, which is shorter than its diff:
```python
import functools

import jax
import jax.numpy as jnp
from jax import lax
from jax.experimental import pallas as pl
from jax.experimental.pallas import tpu as pltpu
from jax.sharding import PartitionSpec as P

EPS = 1e-5
MESH = pl.DeviceIdType.MESH
HBM = pl.BlockSpec(memory_space=pl.ANY)
VMEM = pl.BlockSpec(memory_space=pltpu.VMEM)
F = 4
E = 4
CHUNKS = 8


O_SLOTS = 4
COLS = 8


def moe_kernel(hid, pos, gain, wg, wu, wd, back, hall, full, rows,
               wbuf, xbuf, obuf, hbuf, acc_a, acc_b, pick, tok, out,
               hy_s, hy_r, hs_s, hs_r, hf_s, hf_r, zr_s, zl_s, z_r, x_s, x_r,
               w_sem, x_sem, o_sem, r_sem, t_sem, g_sem):
    half, z, j = lax.axis_index('dp'), lax.axis_index('fsdp'), lax.axis_index('ep')
    y, core = j // 2, j % 2
    sib = j + 1 - 2 * core
    across = (j + 2) % E
    experts, ff, width = wg.shape
    part = width // 2
    tokens, d_model = hid.shape
    capacity = hbuf.shape[0]
    pair = 2 * capacity
    chunk = tokens // CHUNKS
    cols = d_model // COLS
    local = (wg, wu, wd)
    group = 3 * experts // 2
    steps = (F - 1) * group
    blocks = experts * E

    def region(p, f, h):
        return full.at[p % 3, p // 3, :, pl.ds(pl.multiple_of(f * width + h * part, 128), part)]

    def own(p):
        return local[p % 3].at[p // 3, :, pl.ds(pl.multiple_of(half * part, 128), part)]

    def along_z(p, f, src, step, sems):
        return pltpu.make_async_remote_copy(
            src_ref=src, dst_ref=region(p, f, half), send_sem=sems.at[p, f], recv_sem=z_r.at[p, f],
            device_id={'fsdp': z + step}, device_id_type=MESH)

    def along_x(p, f, h):
        return pltpu.make_async_remote_copy(
            src_ref=region(p, f, h), dst_ref=region(p, f, h), send_sem=x_s.at[p, f], recv_sem=x_r.at[p, f],
            device_id={'dp': 1 - half}, device_id_type=MESH)

    def own_start(lo, hi):
        for p in range(lo, hi):
            pl.when(z < F - 1)(lambda p=p: along_z(p, z, own(p), 1, zr_s).start())
            pl.when(z > 0)(lambda p=p: along_z(p, z, own(p), -1, zl_s).start())

    def arrive(p, d):
        def from_left():
            f = z - d
            along_z(p, f, region(p, f, half), 1, zr_s).wait_recv()
            pl.when(z < F - 1)(lambda: along_z(p, f, region(p, f, half), 1, zr_s).start())
            along_x(p, f, half).start()

        def from_right():
            f = z + d
            along_z(p, f, region(p, f, half), 1, zr_s).wait_recv()
            pl.when(z > 0)(lambda: along_z(p, f, region(p, f, half), -1, zl_s).start())
            along_x(p, f, half).start()

        pl.when(z >= d)(from_left)
        pl.when(z < F - d)(from_right)

    def arrivals(base, lo, hi):
        def body(i, c):
            arrive(base + i % group, i // group + 1)
            return c
        lax.fori_loop(lo, hi, body, 0)

    def each_piece(lo, hi, act):
        def body(i, c):
            p, f = lo + i // F, i % F
            act(p, f)
            return c
        lax.fori_loop(0, (hi - lo) * F, body, 0)

    def swapped(lo, hi):
        each_piece(lo, hi, lambda p, f: pl.when(z != f)(lambda: along_x(p, f, 1 - half).wait_recv()))

    def token_copy(src, owner, c, send, recv, target):
        return pltpu.make_async_remote_copy(
            src_ref=src, dst_ref=hall.at[owner, pl.ds(c * chunk, chunk)], send_sem=send.at[c], recv_sem=recv.at[c],
            device_id={'ep': target}, device_id_type=MESH)

    def mine(c):
        return hid.at[pl.ds(c * chunk, chunk)]

    def forward(lo, hi):
        for c in range(lo, hi):
            token_copy(mine(c), across, c, hy_s, hy_r, across).wait_recv()
            token_copy(hall.at[across, pl.ds(c * chunk, chunk)], across, c, hf_s, hf_r, sib).start()

    def device(ybit, cbit):
        return (y + ybit) % 2 * 2 + (core + cbit) % 2

    def token_load(r, n):
        owner = device(r // 4, r % 2)
        ns = pl.ds(pl.multiple_of(n * cols, 128), cols)
        near = pltpu.make_async_copy(hid.at[:, ns], tok.at[n % 2], t_sem.at[n % 2])
        far = pltpu.make_async_copy(hall.at[owner, :, ns], tok.at[n % 2], t_sem.at[n % 2])
        return near, far, r // 4 + r % 2 == 0

    def token_start(r, n):
        near, far, is_near = token_load(r, n)
        pl.when(is_near)(lambda: near.start())
        pl.when(jnp.logical_not(is_near))(lambda: far.start())

    def row_store(r, n):
        ns = pl.ds(pl.multiple_of(n * cols, 128), cols)
        dst = rows.at[r // 4 * 2 + r % 2, pl.ds(pl.multiple_of(r // 2 % 2 * pair, 16), pair), ns]
        return pltpu.make_async_copy(out.at[n % 2], dst, g_sem.at[n % 2])

    def pick_rows(r):
        token_start(r, 0)
        owner = device(r // 4, r % 2)
        step = 32 if capacity % 32 == 0 else capacity

        def mark(i, c):
            e = i // (capacity // step)
            first = (i % (capacity // step)) * step
            want = pos[owner * experts + r // 2 % 2 * 2 + e]
            slot = first + lax.broadcasted_iota(jnp.int32, (step, tokens), 0)
            pick[pl.ds(pl.multiple_of(i * step, step), step), :] = jnp.where(slot == want, 1.0, 0.0).astype(jnp.bfloat16)
            return c
        lax.fori_loop(0, pair // step, mark, 0)

        def column(n, c):
            near, _, _ = token_load(r, n)
            near.wait()
            pl.when(n + 1 < COLS)(lambda: token_start(r, n + 1))
            pl.when(n >= 2)(lambda: row_store(r, n - 2).wait())
            out[n % 2] = jnp.dot(pick[...], tok[n % 2], preferred_element_type=jnp.float32).astype(jnp.bfloat16)
            row_store(r, n).start()
            return c
        lax.fori_loop(0, COLS, column, 0)
        row_store(r, COLS - 2).wait()
        row_store(r, COLS - 1).wait()

    def weights(e, act):
        slot = e % 2
        for t in range(3):
            for f in range(F):
                fs = pl.ds(f * width, width)
                dst, sem = wbuf.at[slot, t, :, fs], w_sem.at[slot, t * F + f]
                pl.when(z == f)(lambda: act(pltpu.make_async_copy(local[t].at[e], dst, sem)))
                pl.when(z != f)(lambda: act(pltpu.make_async_copy(full.at[t, e, :, fs], dst, sem)))

    def start(copy):
        copy.start()

    def wait(copy):
        copy.wait()

    def place(k):
        m = k - 8
        e = jnp.where(k < 4, k // 2, jnp.where(k < 8, k % 2, 2 + m // 4))
        ybit = jnp.where(k < 4, 0, jnp.where(k < 8, 1, 1 - m % 2))
        cbit = jnp.where(k < 4, k % 2, jnp.where(k < 8, (k - 4) // 2, m % 4 // 2))
        return e, ybit, cbit

    def x_load(k):
        e, ybit, cbit = place(k)
        src = rows.at[ybit * 2 + cbit, pl.ds(pl.multiple_of(e * capacity, 16), capacity)]
        return pltpu.make_async_copy(src, xbuf.at[k % 2], x_sem.at[k % 2])

    def send(k):
        e, ybit, cbit = place(k)
        return pltpu.make_async_remote_copy(
            src_ref=obuf.at[k % O_SLOTS], dst_ref=back.at[j * experts + e], send_sem=o_sem.at[k % O_SLOTS],
            recv_sem=r_sem.at[j * experts + e], device_id={'ep': device(ybit, cbit)}, device_id_type=MESH)

    def keep(k):
        e, _, _ = place(k)
        return pltpu.make_async_copy(obuf.at[k % O_SLOTS], back.at[j * experts + e], o_sem.at[k % O_SLOTS])

    def is_local(k):
        _, ybit, cbit = place(k)
        return ybit + cbit == 0

    def sent(k):
        pl.when(is_local(k))(lambda: keep(k).wait())
        pl.when(jnp.logical_not(is_local(k)))(lambda: send(k).wait_send())

    def block(k, last):
        e, _, _ = place(k)
        slot, xs, os = e % 2, k % 2, k % O_SLOTS
        pl.when(k < 4)(lambda: arrivals(group, k, k + 1))
        for at, lo, hi in ((4, 5, 8), (5, 8, 9), (6, 9, 11), (7, 11, 13)):
            pl.when(k == at)(lambda: arrivals(group, lo, hi))

        @pl.when(k == 8)
        def _():
            arrivals(group, 13, steps)
            swapped(group, 2 * group)
            weights(2, start)
            weights(3, start)
            weights(2, wait)
        pl.when(k == 0)(lambda: weights(0, wait))
        pl.when(k == 2)(lambda: weights(1, wait))
        pl.when(k == 12)(lambda: weights(3, wait))

        x_load(k).wait()
        pl.when(k + 1 < last)(lambda: x_load(k + 1).start())

        step = 16 if capacity % 16 == 0 else capacity
        def norm(r, c):
            rs = pl.ds(pl.multiple_of(r * step, step), step)
            x = xbuf[xs, rs, :].astype(jnp.float32)
            scale = lax.rsqrt(jnp.mean(x * x, axis=-1, keepdims=True) + EPS)
            xbuf[xs, rs, :] = (x * scale * gain[...]).astype(jnp.bfloat16)
            return c
        lax.fori_loop(0, capacity // step, norm, 0)

        acc_a[...] = jnp.zeros_like(acc_a)
        acc_b[...] = jnp.zeros_like(acc_b)
        def first(i, c):
            ks = pl.ds(pl.multiple_of(i * width, 128), width)
            u = xbuf[xs, :, ks]
            dims = (((1,), (1,)), ((), ()))
            acc_a[...] += lax.dot_general(u, wbuf[slot, 0, :, ks], dims, preferred_element_type=jnp.float32)
            acc_b[...] += lax.dot_general(u, wbuf[slot, 1, :, ks], dims, preferred_element_type=jnp.float32)
            return c
        lax.fori_loop(0, F, first, 0)
        a = acc_a[...]
        hbuf[...] = (a * jax.nn.sigmoid(a) * acc_b[...]).astype(jnp.bfloat16)

        pl.when(k >= O_SLOTS)(lambda: sent(k - O_SLOTS))
        def second(i, c):
            ns = pl.ds(pl.multiple_of(i * width, 128), width)
            obuf[os, :, ns] = jnp.dot(
                hbuf[...], wbuf[slot, 2, :, ns], preferred_element_type=jnp.float32).astype(jnp.bfloat16)
            return c
        lax.fori_loop(0, F, second, 0)
        pl.when(is_local(k))(lambda: keep(k).start())
        pl.when(jnp.logical_not(is_local(k)))(lambda: send(k).start())
        return last

    for c in range(CHUNKS):
        token_copy(mine(c), j, c, hs_s, hs_r, sib).start()
        token_copy(mine(c), j, c, hy_s, hy_r, across).start()
    own_start(0, group)

    def round_(r, c):
        @pl.when(r == 1)
        def _():
            for c in range(CHUNKS):
                token_copy(mine(c), sib, c, hs_s, hs_r, sib).wait_recv()

        @pl.when(r == 4)
        def _():
            forward(6, CHUNKS)
            arrivals(group, 4, 5)

        @pl.when(r == 5)
        def _():
            for c in range(CHUNKS):
                token_copy(mine(c), sib, c, hf_s, hf_r, sib).wait_recv()

        pick_rows(r)
        pl.when(r == 1)(lambda: arrivals(0, 0, 2))
        pl.when(r == 2)(lambda: arrivals(0, 2, 4))

        @pl.when(r == 3)
        def _():
            arrivals(0, 4, 6)
            forward(0, 2)
            arrivals(0, 6, 9)
            forward(2, 3)
            arrivals(0, 9, 12)
            forward(3, 4)
            own_start(group, 2 * group)
            arrivals(0, 12, 15)
            forward(4, 5)
            arrivals(0, 15, steps)
            forward(5, 6)
            swapped(0, group)
            weights(0, start)
            weights(1, start)

        def upto(r):
            return (jnp.where(r >= 3, 4, 0) + jnp.where(r >= 4, 2, 0) + jnp.where(r >= 5, 2, 0) + jnp.where(r >= 7, 8, 0))
        lo, hi = upto(r - 1), upto(r)
        pl.when(lo < hi)(lambda: x_load(lo).start())
        lax.fori_loop(lo, hi, lambda k, last: block(k, last), hi)
        return c

    lax.fori_loop(0, 8, round_, 0)

    for k in range(blocks - O_SLOTS, blocks):
        sent(jnp.int32(k))
    for c in range(CHUNKS):
        token_copy(mine(c), j, c, hy_s, hy_r, across).wait_send()
        token_copy(mine(c), j, c, hs_s, hs_r, sib).wait_send()
        token_copy(mine(c), j, c, hf_s, hf_r, sib).wait_send()

    def drain(p, f):
        src = region(p, f, half)
        pl.when(jnp.logical_and(z < F - 1, f <= z))(lambda: along_z(p, f, src, 1, zr_s).wait_send())
        pl.when(jnp.logical_and(z > 0, f >= z))(lambda: along_z(p, f, src, -1, zl_s).wait_send())
        pl.when(z != f)(lambda: along_x(p, f, half).wait_send())
    each_piece(0, 2 * group, drain)

    def arrived(n, c):
        def wait_block():
            pltpu.make_async_remote_copy(
                src_ref=obuf.at[0], dst_ref=back.at[n], send_sem=o_sem.at[0], recv_sem=r_sem.at[n],
                device_id={'ep': n // experts}, device_id_type=MESH).wait_recv()
        pl.when(n // experts != j)(wait_block)
        return c
    lax.fori_loop(0, blocks, arrived, 0)


def run_moe(hidden, positions, gain, w_gate, w_up, w_down, capacity):
    tokens, d_model = hidden.shape
    experts, ff, width = w_gate.shape
    bf16, f32, dma = jnp.bfloat16, jnp.float32, pltpu.SemaphoreType.DMA
    pieces = 3 * experts
    shapes = (
        (E * experts, capacity, d_model),
        (E, tokens, d_model),
        (3, experts, ff, d_model),
        (E, experts * capacity, d_model),
    )
    return pl.pallas_call(
        moe_kernel,
        out_shape=tuple(jax.ShapeDtypeStruct(shape, bf16) for shape in shapes),
        in_specs=[HBM, VMEM, VMEM] + [HBM] * 3,
        out_specs=(HBM,) * 4,
        scratch_shapes=[
            pltpu.VMEM((2, 3, ff, d_model), bf16),
            pltpu.VMEM((2, capacity, d_model), bf16),
            pltpu.VMEM((O_SLOTS, capacity, d_model), bf16),
            pltpu.VMEM((capacity, ff), bf16),
            pltpu.VMEM((capacity, ff), f32),
            pltpu.VMEM((capacity, ff), f32),
            pltpu.VMEM((2 * capacity, tokens), bf16),
            pltpu.VMEM((2, tokens, d_model // COLS), bf16),
            pltpu.VMEM((2, 2 * capacity, d_model // COLS), bf16),
        ] + [dma((CHUNKS,)) for _ in range(6)] + [dma((pieces, F)) for _ in range(5)] + [
            dma((2, 3 * F)), dma((2,)), dma((O_SLOTS,)), dma((E * experts,)), dma((2,)), dma((2,)),
        ],
        compiler_params=pltpu.CompilerParams(has_side_effects=True, vmem_limit_bytes=63 * 1024 * 1024),
        name='moe',
    )(hidden, positions, gain, w_gate, w_up, w_down)[0]


def gate_values(hidden_f32, norm_gain, w_router, top2_ids):
    mean_sq = jnp.mean(hidden_f32 * hidden_f32, axis=-1, keepdims=True)
    normed = (hidden_f32 * lax.rsqrt(mean_sq + EPS) * norm_gain.astype(jnp.float32)).astype(jnp.bfloat16)
    logits = jnp.dot(normed, w_router, preferred_element_type=jnp.float32)
    experts = jnp.arange(w_router.shape[1], dtype=jnp.int32)
    picked = [jnp.sum(jnp.where(top2_ids[:, k:k + 1] == experts, logits, 0.0), axis=1) for k in range(2)]
    return jax.nn.softmax(jnp.stack(picked, axis=1), axis=-1)


def local_block(hidden, norm_gain, w_router, w_gate, w_up, w_down, top2_ids):
    tok_local, d_model = hidden.shape
    num_experts = w_router.shape[1]
    capacity = (5 * tok_local + 2 * num_experts - 1) // (2 * num_experts)
    experts = num_experts // E

    ids = [top2_ids[:, k][None, :] for k in range(2)]
    expert_ids = jnp.arange(num_experts, dtype=jnp.int32)[:, None]
    chosen = jnp.logical_or(ids[0] == expert_ids, ids[1] == expert_ids)
    before = jnp.cumsum(chosen.astype(jnp.int32), axis=1) - 1
    positions = jnp.where(chosen, before, -1)
    place = [jnp.sum(jnp.where(ids[k] == expert_ids, before, 0), axis=0) for k in range(2)]
    positions = lax.all_to_all(positions.reshape(E, experts, tok_local), 'ep', 0, 0)
    positions = positions.reshape(E * experts, 1, tok_local)

    gain = norm_gain.astype(jnp.float32).reshape(1, d_model)
    back = run_moe(hidden, positions, gain, jnp.swapaxes(w_gate, 1, 2), jnp.swapaxes(w_up, 1, 2), w_down, capacity)
    back = back.reshape(num_experts * capacity, d_model)

    hidden_f32 = hidden.astype(jnp.float32)
    gate_probs = gate_values(hidden_f32, norm_gain, w_router, top2_ids)
    moe = []
    for k in range(2):
        returned = jnp.take(back, top2_ids[:, k] * capacity + place[k], axis=0, mode='clip').astype(jnp.float32)
        moe.append(jnp.where((place[k] < capacity)[:, None], gate_probs[:, k:k + 1] * returned, 0.0))
    return (hidden_f32 + (moe[0] + moe[1])).astype(jnp.bfloat16)


def solution(mesh):
    tok_spec = P(('dp', 'fsdp', 'ep'), None)
    in_specs = (tok_spec, P(None), P(None, None), P('ep', 'fsdp', None), P('ep', 'fsdp', None), P('ep', None, 'fsdp'), tok_spec)
    return jax.shard_map(local_block, mesh=mesh, in_specs=in_specs, out_specs=tok_spec, check_vma=False)
```

time: 2130 us -> 1060 us (0.50)
  waiting for transfers between devices: 1280 us -> 0.01 us
  Pallas kernels: 0 us -> 868 us
  local copies, waits for them, and re-layouts: 463 us -> 135 us
  other arithmetic: 200 us -> 43 us
  matrix products: 137 us -> 8.19 us
    pallas_call x0 -> x1, Pallas kernels: none -> 868 us  [run_moe(): pl.pallas_call(moe_kernel, out_shape=tuple((jax.ShapeDtypeStruct(shape, b...]
    all_to_all x2 -> x1, waiting for transfers between devices: 853 us -> 0.01 us  [local_block(): lax.all_to_all(positions.reshape(E, experts, tok_local), 'ep', 0, 0)]
    all_gather x3 -> x0, waiting for transfers between devices: 424 us -> none  [the longest x1 340 us: local_block(): down_full = lax.all_gather(w_down, 'fsdp', axis=2, tiled=True)]
    gather x8 -> x2, local copies, waits for them, and re-layouts: 320 us -> 133 us  [local_block(): jnp.take(back, top2_ids[:, k] * capacity + place[k], axis=0, mode='clip')]
    dot_general x4 -> x1, matrix products: 137 us -> 8.19 us  [gate_values(): logits = jnp.dot(normed, w_router, preferred_element_type=jnp.float32)]
    reduce_sum x4 -> x3, other arithmetic: 134 us -> 7.36 us  [the longest x1 7.21 us: gate_values(): mean_sq = jnp.mean(hidden_f32 * hidden_f32, axis=-1, keepdims=True)]
    all_to_all x2 -> x0, local copies, waits for them, and re-layouts: 64.1 us -> none  [the longest x1 36.1 us: local_block(): back_rows = lax.all_to_all(expert_out, 'ep', 1, 0, tiled=True)]
    convert_element_type x1 -> x0, local copies, waits for them, and re-layouts: 52 us -> none  [expert_block(): jnp.einsum('ecf,efd->ecd', hidden_act, down_full, preferred_element_type=...]
  transfers between devices with their start and end apart: 5 -> 1, of which waited for: 4 -> 0; matrix products, arithmetic and copies ran while one was open for 15% -> 2% of each run, Pallas kernels for 0% -> 0%
where the time goes in v2:
time: 1060 us
  Pallas kernels  868 us (82%)
  local copies, waits for them, and re-layouts  135 us (13%)
  other arithmetic  43 us (4%)
    pallas_call x1, Pallas kernels, run_moe(): pl.pallas_call(moe_kernel, out_shape=tuple((jax.ShapeDtypeStruct(shape, b...  868 us
    gather x2, local copies, waits for them, and re-layouts, local_block(): jnp.take(back, top2_ids[:, k] * capacity + place[k], axis=0, mode='clip')  133 us
    convert_element_type x1, other arithmetic, local_block(): return (hidden_f32 + (moe[0] + moe[1])).astype(jnp.bfloat16)  28.5 us
  transfers between devices with their start and end apart: 1, of which 0 were waited for; matrix products, arithmetic and copies ran while one was open for 2% of the time, Pallas kernels for 0%

profile of v2, /device:TPU:1, one launch (start us, length us, event | category | flops | bytes accessed | tf_op | source)
XLA Modules:
  0.0 1058.2 jit_solution(17471254522288794990)
XLA Ops:
  0.0 0.0 copy-start
  0.0 0.8 fusion.13
  0.9 4.5 reduce-window.6
  5.4 0.4 slice_reduce_fusion
  5.8 0.2 reduce-window.9
  6.0 0.1 select_reduce_fusion.3
  6.2 0.8 or_select_fusion
  6.9 4.3 all-to-all-start
  11.2 0.7 convert_element_type.25
  11.9 0.0 copy-start.2
  11.9 0.8 multiply_add_fusion.1
  12.8 7.2 fusion
  20.0 0.0 copy-done
  20.0 8.2 select_reduce_fusion.1
  28.3 0.0 all-to-all-done
  28.4 0.8 reshape.122.pos
  29.2 0.0 copy-done.2
  29.2 867.5 %moe.1 = (bf16[16,320,4096]{2,1,0:T(8,128)(2,1)}, bf16[4,2048,4096]{2,1,0:T(8,128)(2,1)}, bf16[3,4,688,4096]{3,2,1,0:T(8,128)(2,1)}, bf16[4,1280,4096]{2,1,0:T(8,128)(2,1)}) custom-call(bf16[2048,4096]{1,0:T(8,128)(2,1)} %hid.1, s32[16,1,2048]{2,1,0:T(1,128)} %reshape.122.pos, f32[1,4096]{1,0:T(1,128)} %bitcast.40, bf16[4,688,1024]{2,1,0:T(8,128)(2,1)} %bitcast.24, ...), custom_call_target="tpu_custom_call" | custom-call | tf_op jit(solution)/shard_map/moe/pallas_call | solution.py:340
  896.7 66.3 %gather_fusion.1 = bf16[2048,4096]{1,0:T(8,128)(2,1)} fusion(bf16[5120,4096]{1,0:T(8,128)(2,1)} %bitcast.22, s32[2048]{0:T(1024)S(1)} %broadcast_clamp_fusion), kind=kCustom, calls=%fused_computation.1 | custom fusion | bytes 33562624 | tf_op jit(solution)/shard_map/jit(_take)/gather | solution.py:395
  963.0 66.6 %gather_fusion = bf16[2048,4096]{1,0:T(8,128)(2,1)} fusion(bf16[5120,4096]{1,0:T(8,128)(2,1)} %bitcast.23, s32[2048]{0:T(1024)S(1)} %broadcast_clamp_fusion.1), kind=kCustom, calls=%fused_computation | custom fusion | bytes 33562624 | tf_op jit(solution)/shard_map/jit(_take)/gather | solution.py:395
  1029.7 0.0 copy-start.1
  1029.7 28.5 %fusion.3 = bf16[2048,4096]{1,0:T(8,128)(2,1)} fusion(bf16[2048,4096]{1,0:T(8,128)(2,1)} %hid.1, bf16[2048,4096]{1,0:T(8,128)(2,1)} %gather_fusion.1, bf16[2048,4096]{1,0:T(8,128)(2,1)} %gather_fusion, f32[2048]{0:T(1024)S(1)} %bitcast.42, f32[2048]{0:T(1024)S(1)} %bitcast.41, pred[2048]{0:T(1024)(128)(4,1)S(1)} %get-tuple-element.18, ...), kind=kLoop, calls=%fused_computation.8 | loop fusion | flops 83886080 | bytes 67129344 | tf_op jit(solution)/shard_map/convert_element_type | solution.py:397
  1058.2 0.0 copy-done.1
  (11 shorter events, 0.2 us)
Async XLA Ops:
  0.0 20.0 %copy-start = (bf16[4096,16]{0,1:T(8,128)(2,1)S(1)}, bf16[4096,16]{0,1:T(8,128)(2,1)}, u32[]{:S(2)}) copy-start(bf16[4096,16]{0,1:T(8,128)(2,1)} %param.9) | copy-start | bytes 393220
  6.9 21.4 %all-to-all-start = ((s32[4,4,2048]{2,1,0:T(4,128)}), s32[4,4,2048]{2,1,0:T(4,128)S(1)}, u32[]{:S(2)}, u32[]{:S(2)}) async-start(s32[4,4,2048]{2,1,0:T(4,128)} %or_select_fusion), calls=%async_computation | async-start | bytes 262144 | tf_op jit(solution)/shard_map/all_to_all | solution.py:384
  11.9 17.3 %copy-start.2 = (f32[4096]{0:T(1024)}, f32[4096]{0:T(1024)S(1)}, u32[]{:S(2)}) copy-start(f32[4096]{0:T(1024)S(1)} %convert_element_type.25) | copy-start | bytes 49156
  1029.7 28.5 %copy-start.1 = (bf16[4096,16]{0,1:T(8,128)(2,1)S(1)}, bf16[4096,16]{0,1:T(8,128)(2,1)}, u32[]{:S(2)}) copy-start(bf16[4096,16]{0,1:T(8,128)(2,1)} %param.9) | copy-start | bytes 393220

commit v3 on v2

--- a/solution.py
+++ b/solution.py
@@ -360,6 +360,107 @@
     )(hidden, positions, gain, w_gate, w_up, w_down)[0]
 
 
+TILE = 128
+SPAN = 16
+WINDOWS = 32
+
+
+def combine_kernel(starts, slots, probs, hid, back, out, buf, base, count, acc, sem):
+    i = pl.program_id(0)
+    num_experts = starts.shape[0] // (pl.num_programs(0) + 1)
+    capacity = back.shape[0] // num_experts
+    d_model = back.shape[1]
+    cols = d_model // 4
+
+    def window(row, s, n):
+        src = back.at[pl.ds(pl.multiple_of(row, SPAN), SPAN)]
+        return pltpu.make_async_copy(src, buf.at[s, pl.ds(pl.multiple_of(n * SPAN, SPAN), SPAN)], sem.at[s])
+
+    def fill(tile, turn, s):
+        first = turn * WINDOWS
+
+        def clear(n, c):
+            base[s, n] = -100000
+            return c
+        lax.fori_loop(0, WINDOWS, clear, 0)
+
+        def expert(e, n):
+            lo, hi = starts[tile * num_experts + e], starts[(tile + 1) * num_experts + e]
+
+            def one(c, n):
+                @pl.when(jnp.logical_and(n >= first, n < first + WINDOWS))
+                def _():
+                    row = e * capacity + c * SPAN
+                    base[s, n - first] = row
+                    window(row, s, n - first).start()
+                return n + 1
+            return lax.fori_loop(lo // SPAN, jnp.where(hi > lo, (hi + SPAN - 1) // SPAN, lo // SPAN), one, n)
+        count[s] = lax.fori_loop(0, num_experts, expert, jnp.int32(0))
+
+    def use(turn, s):
+        def arrived(n, c):
+            window(0, s, 0).wait()
+            return c
+        lax.fori_loop(0, jnp.minimum(count[s] - turn * WINDOWS, WINDOWS), arrived, 0)
+        lane = lax.broadcasted_iota(jnp.int32, (1, WINDOWS * SPAN), 1)
+        row = jnp.zeros_like(lane)
+        for n in range(WINDOWS):
+            row = jnp.where(lane // SPAN == n, base[s, n], row)
+        row = row + lane % SPAN
+        pick = jnp.where(slots[0] == row, 1.0, 0.0).astype(jnp.bfloat16)
+        p0, p1 = probs[0, :TILE], probs[0, TILE:]
+
+        def column(n, c):
+            ns = pl.ds(pl.multiple_of(n * cols, 128), cols)
+            got = jnp.dot(pick, buf[s, :, ns], preferred_element_type=jnp.float32)
+            acc[:, ns] += p0 * got[:TILE] + p1 * got[TILE:]
+            return c
+        lax.fori_loop(0, 4, column, 0)
+
+    s = i % 2
+
+    @pl.when(i == 0)
+    def _():
+        buf[...] = jnp.zeros_like(buf)
+        fill(i, 0, s)
+    pl.when(i + 1 < pl.num_programs(0))(lambda: fill(i + 1, 0, 1 - s))
+    acc[...] = hid[...].astype(jnp.float32)
+    use(0, s)
+
+    def more(turn, c):
+        fill(i, turn, s)
+        use(turn, s)
+        return c
+    lax.fori_loop(1, (count[s] + WINDOWS - 1) // WINDOWS, more, 0)
+    out[...] = acc[...].astype(out.dtype)
+
+
+def combine(hidden, back, starts, slots, probs):
+    tokens, d_model = hidden.shape
+    tiles = tokens // TILE
+    column = pl.BlockSpec((1, 2 * TILE, 1), lambda i: (i, 0, 0))
+    row = pl.BlockSpec((TILE, d_model), lambda i: (i, 0))
+
+    def by_tile(x):
+        return jnp.swapaxes(x.reshape(2, tiles, TILE), 0, 1).reshape(tiles, 2 * TILE, 1)
+    return pl.pallas_call(
+        combine_kernel,
+        grid=(tiles,),
+        out_shape=jax.ShapeDtypeStruct(hidden.shape, hidden.dtype),
+        in_specs=[pl.BlockSpec(memory_space=pltpu.SMEM), column, column, row, HBM],
+        out_specs=row,
+        scratch_shapes=[
+            pltpu.VMEM((2, WINDOWS * SPAN, d_model), jnp.bfloat16),
+            pltpu.SMEM((2, WINDOWS), jnp.int32),
+            pltpu.SMEM((2,), jnp.int32),
+            pltpu.VMEM((TILE, d_model), jnp.float32),
+            pltpu.SemaphoreType.DMA((2,)),
+        ],
+        compiler_params=pltpu.CompilerParams(dimension_semantics=('arbitrary',)),
+        name='combine',
+    )(starts.reshape(-1), by_tile(slots), by_tile(probs), hidden, back)
+
+
 def gate_values(hidden_f32, norm_gain, w_router, top2_ids):
     mean_sq = jnp.mean(hidden_f32 * hidden_f32, axis=-1, keepdims=True)
     normed = (hidden_f32 * lax.rsqrt(mean_sq + EPS) * norm_gain.astype(jnp.float32)).astype(jnp.bfloat16)
@@ -388,13 +489,11 @@
     back = run_moe(hidden, positions, gain, jnp.swapaxes(w_gate, 1, 2), jnp.swapaxes(w_up, 1, 2), w_down, capacity)
     back = back.reshape(num_experts * capacity, d_model)
 
-    hidden_f32 = hidden.astype(jnp.float32)
-    gate_probs = gate_values(hidden_f32, norm_gain, w_router, top2_ids)
-    moe = []
-    for k in range(2):
-        returned = jnp.take(back, top2_ids[:, k] * capacity + place[k], axis=0, mode='clip').astype(jnp.float32)
-        moe.append(jnp.where((place[k] < capacity)[:, None], gate_probs[:, k:k + 1] * returned, 0.0))
-    return (hidden_f32 + (moe[0] + moe[1])).astype(jnp.bfloat16)
+    gate_probs = gate_values(hidden.astype(jnp.float32), norm_gain, w_router, top2_ids)
+    slots = jnp.stack([jnp.where(place[k] < capacity, top2_ids[:, k] * capacity + place[k], -1) for k in range(2)])
+    counts = jnp.minimum(before[:, TILE - 1::TILE].T + 1, capacity)
+    starts = jnp.concatenate([jnp.zeros((1, num_experts), jnp.int32), counts], axis=0)
+    return combine(hidden, back, starts, slots, gate_probs.T)
 
 
 def solution(mesh):

time: 1060 us -> 977 us (0.922)
  local copies, waits for them, and re-layouts: 135 us -> 13 us
  Pallas kernels: 868 us -> 932 us
  other arithmetic: 43 us -> 13.2 us
    gather x2 -> x0, local copies, waits for them, and re-layouts: 133 us -> none  [local_block(): jnp.take(back, top2_ids[:, k] * capacity + place[k], axis=0, mode='clip')]
    pallas_call x0 -> x1, Pallas kernels: none -> 64.3 us  [combine(): pl.pallas_call(combine_kernel, grid=(tiles,), out_shape=jax.ShapeDtypeStr...]
    convert_element_type x1 -> x0, other arithmetic: 28.5 us -> none  [local_block(): return (hidden_f32 + (moe[0] + moe[1])).astype(jnp.bfloat16)]
where the time goes in v3:
time: 977 us; the launch traced here: 968 us
  Pallas kernels  932 us (95%)
  other arithmetic  13.2 us (1%)
  local copies, waits for them, and re-layouts  13 us (1%)
    pallas_call x1, Pallas kernels, run_moe(): pl.pallas_call(moe_kernel, out_shape=tuple((jax.ShapeDtypeStruct(shape, b...  868 us
    pallas_call x1, Pallas kernels, combine(): pl.pallas_call(combine_kernel, grid=(tiles,), out_shape=jax.ShapeDtypeStr...  64.3 us
  transfers between devices with their start and end apart: 1, of which 0 were waited for; matrix products, arithmetic and copies ran while one was open for 2% of the time, Pallas kernels for 0%

profile of v3, /device:TPU:1, one launch (start us, length us, event | category | flops | bytes accessed | tf_op | source)
XLA Modules:
  0.0 967.6 jit_solution(6428110269278106255)
XLA Ops:
  0.0 0.0 copy-start
  0.0 0.0 copy-start.5
  0.0 0.8 fusion.11
  0.9 4.5 reduce-window.6
  5.4 0.4 slice_reduce_fusion
  5.8 0.2 reduce-window.9
  6.0 0.1 select_reduce_fusion.3
  6.2 0.8 or_select_fusion
  6.9 4.3 all-to-all-start
  11.2 0.3 copy.16
  11.6 0.0 copy-start.2
  11.6 7.5 fusion
  19.0 0.0 copy-start.4
  19.1 0.0 copy-done.5
  19.1 0.0 copy-done
  19.1 3.1 copy-done.2
  22.2 0.0 copy-start.3
  22.2 4.9 select_reduce_fusion
  27.4 0.6 reshape.176.starts
  28.0 0.0 copy-done.4
  28.1 3.3 reshape.182.slots
  31.4 0.0 copy-done.3
  31.4 3.3 reshape.183.probs
  34.7 0.0 all-to-all-done
  34.7 0.8 reshape.180.pos
  35.6 867.5 %moe.1 = (bf16[16,320,4096]{2,1,0:T(8,128)(2,1)}, bf16[4,2048,4096]{2,1,0:T(8,128)(2,1)}, bf16[3,4,688,4096]{3,2,1,0:T(8,128)(2,1)}, bf16[4,1280,4096]{2,1,0:T(8,128)(2,1)}) custom-call(bf16[2048,4096]{1,0:T(8,128)(2,1)} %hid.3, s32[16,1,2048]{2,1,0:T(1,128)} %reshape.180.pos, f32[1,4096]{1,0:T(1,128)} %bitcast.56, bf16[4,688,1024]{2,1,0:T(8,128)(2,1)} %bitcast.41, ...), custom_call_target="tpu_custom_call" | custom-call | tf_op jit(solution)/shard_map/moe/pallas_call | solution.py:340
  903.1 0.0 copy-start.1
  903.1 64.3 %combine.1 = bf16[2048,4096]{1,0:T(8,128)(2,1)} custom-call(s32[272]{0:T(512)} %reshape.176.starts, s32[16,256,1]{2,1,0:T(8,128)} %reshape.182.slots, f32[16,256,1]{2,1,0:T(8,128)} %reshape.183.probs, bf16[2048,4096]{1,0:T(8,128)(2,1)} %hid.3, bf16[5120,4096]{1,0:T(8,128)(2,1)} %bitcast.40), custom_call_target="tpu_custom_call" | custom-call | tf_op jit(solution)/shard_map/combine/pallas_call | solution.py:446
  967.4 0.0 copy-done.1
  (15 shorter events, 0.3 us)
Async XLA Ops:
  0.0 19.1 %copy-start = (bf16[4096,16]{0,1:T(8,128)(2,1)S(1)}, bf16[4096,16]{0,1:T(8,128)(2,1)}, u32[]{:S(2)}) copy-start(bf16[4096,16]{0,1:T(8,128)(2,1)} %param.9) | copy-start | bytes 393220
  0.0 19.1 %copy-start.5 = (bf16[4096]{0:T(1024)(128)(2,1)S(1)}, bf16[4096]{0:T(1024)(128)(2,1)}, u32[]{:S(2)}) copy-start(bf16[4096]{0:T(1024)(128)(2,1)} %param.8) | copy-start | bytes 24580
  6.9 27.8 %all-to-all-start = ((s32[4,4,2048]{2,1,0:T(4,128)}), s32[4,4,2048]{2,1,0:T(4,128)S(1)}, u32[]{:S(2)}, u32[]{:S(2)}) async-start(s32[4,4,2048]{2,1,0:T(4,128)} %or_select_fusion), calls=%async_computation | async-start | bytes 262144 | tf_op jit(solution)/shard_map/all_to_all | solution.py:485
  11.6 10.7 %copy-start.2 = (bf16[2048,4096]{1,0:T(8,128)(2,1)S(1)}, bf16[2048,4096]{1,0:T(8,128)(2,1)}, u32[]{:S(2)}) copy-start(bf16[2048,4096]{1,0:T(8,128)(2,1)} %hid.3) | copy-start | bytes 50331652
  19.0 9.0 copy-start.4
  22.2 9.2 copy-start.3
  903.1 64.3 %copy-start.1 = (bf16[4096,16]{0,1:T(8,128)(2,1)S(1)}, bf16[4096,16]{0,1:T(8,128)(2,1)}, u32[]{:S(2)}) copy-start(bf16[4096,16]{0,1:T(8,128)(2,1)} %param.9) | copy-start | bytes 393220

commit v4 on v3

--- a/solution.py
+++ b/solution.py
@@ -20,10 +20,10 @@
 COLS = 8
 
 
-def moe_kernel(hid, pos, gain, wg, wu, wd, back, hall, full, rows,
-               wbuf, xbuf, obuf, hbuf, acc_a, acc_b, pick, tok, out,
+def moe_kernel(hid, pos, gain, router, wg, wu, wd, back, hall, full, rows, logits,
+               wbuf, xbuf, obuf, hbuf, acc_a, acc_b, pick, tok, out, squares,
                hy_s, hy_r, hs_s, hs_r, hf_s, hf_r, zr_s, zl_s, z_r, x_s, x_r,
-               w_sem, x_sem, o_sem, r_sem, t_sem, g_sem):
+               w_sem, x_sem, o_sem, r_sem, t_sem, g_sem, l_sem):
     half, z, j = lax.axis_index('dp'), lax.axis_index('fsdp'), lax.axis_index('ep')
     y, core = j // 2, j % 2
     sib = j + 1 - 2 * core
@@ -35,6 +35,7 @@
     pair = 2 * capacity
     chunk = tokens // CHUNKS
     cols = d_model // COLS
+    early = tokens - chunk
     local = (wg, wu, wd)
     group = 3 * experts // 2
     steps = (F - 1) * group
@@ -126,8 +127,7 @@
         dst = rows.at[r // 4 * 2 + r % 2, pl.ds(pl.multiple_of(r // 2 % 2 * pair, 16), pair), ns]
         return pltpu.make_async_copy(out.at[n % 2], dst, g_sem.at[n % 2])
 
-    def pick_rows(r):
-        token_start(r, 0)
+    def mark_rows(r):
         owner = device(r // 4, r % 2)
         step = 32 if capacity % 32 == 0 else capacity
 
@@ -140,17 +140,89 @@
             return c
         lax.fori_loop(0, pair // step, mark, 0)
 
+    def some_rows(act):
+        step = min(tokens, 256)
+
+        def body(i, c):
+            act(pl.ds(pl.multiple_of(i * step, step), step))
+            return c
+        lax.fori_loop(0, tokens // step, body, 0)
+
+    def route(r, n):
+        ns = pl.ds(pl.multiple_of(n * cols, 128), cols)
+
+        @pl.when(r == 0)
+        def _():
+            def add_squares(rs):
+                x = tok[n % 2, rs, :].astype(jnp.float32)
+                squares[rs, :] += jnp.sum(x * x, axis=-1, keepdims=True)
+            some_rows(add_squares)
+
+        @pl.when(r == 2)
+        def _():
+            def add_logits(rs):
+                x = tok[n % 2, rs, :].astype(jnp.float32)
+                scale = lax.rsqrt(squares[rs, :] / d_model + EPS)
+                u = (x * scale * gain[:, ns]).astype(jnp.bfloat16)
+                logits[rs, :] += lax.dot_general(
+                    u, router[:, ns], (((1,), (1,)), ((), ())), preferred_element_type=jnp.float32)
+            some_rows(add_logits)
+
+    def pick_rows(r):
+        token_start(r, 0)
+        mark_rows(r)
+
         def column(n, c):
-            near, _, _ = token_load(r, n)
-            near.wait()
+            token_load(r, n)[0].wait()
             pl.when(n + 1 < COLS)(lambda: token_start(r, n + 1))
             pl.when(n >= 2)(lambda: row_store(r, n - 2).wait())
             out[n % 2] = jnp.dot(pick[...], tok[n % 2], preferred_element_type=jnp.float32).astype(jnp.bfloat16)
             row_store(r, n).start()
+            route(r, n)
             return c
         lax.fori_loop(0, COLS, column, 0)
         row_store(r, COLS - 2).wait()
         row_store(r, COLS - 1).wait()
+
+    def pick_first_across():
+        def load(n):
+            ns = pl.ds(pl.multiple_of(n * cols, 128), cols)
+            return pltpu.make_async_copy(
+                hall.at[across, pl.ds(0, early), ns], tok.at[n % 2, pl.ds(0, early)], t_sem.at[n % 2])
+
+        def load_last(n):
+            return pltpu.make_async_copy(
+                hall.at[across, pl.ds(early, chunk), pl.ds(n * cols, cols)], tok.at[0, pl.ds(n * chunk, chunk)], l_sem.at[n])
+
+        mark_rows(4)
+        forward(6, CHUNKS - 1)
+        load(0).start()
+        arrivals(group, 4, 5)
+
+        def column(n, c):
+            ns = pl.ds(pl.multiple_of(n * cols, 128), cols)
+            load(n).wait()
+            pl.when(n + 1 < COLS)(lambda: load(n + 1).start())
+            got = jnp.dot(pick[:, :early], tok[n % 2, :early], preferred_element_type=jnp.float32).astype(jnp.bfloat16)
+            xbuf[0, :, ns] = got[:capacity]
+            xbuf[1, :, ns] = got[capacity:]
+            return c
+        lax.fori_loop(0, COLS, column, 0)
+        forward(CHUNKS - 1, CHUNKS)
+        for n in range(COLS):
+            load_last(n).start()
+
+        for n in range(COLS):
+            load_last(n).wait()
+
+        def column_last(n, c):
+            ns = pl.ds(pl.multiple_of(n * cols, 128), cols)
+            rest = tok[0, pl.ds(pl.multiple_of(n * chunk, 16), chunk), :]
+            got = jnp.dot(pick[:, early:], rest, preferred_element_type=jnp.float32).astype(jnp.bfloat16)
+            xbuf[0, :, ns] += got[:capacity]
+            xbuf[1, :, ns] += got[capacity:]
+            return c
+        lax.fori_loop(0, COLS, column_last, 0)
 
     def weights(e, act):
         slot = e % 2
@@ -178,6 +250,9 @@
         e, ybit, cbit = place(k)
         src = rows.at[ybit * 2 + cbit, pl.ds(pl.multiple_of(e * capacity, 16), capacity)]
         return pltpu.make_async_copy(src, xbuf.at[k % 2], x_sem.at[k % 2])
+
+    def from_rows(k):
+        return jnp.logical_or(k < 4, k > 5)
 
     def send(k):
         e, ybit, cbit = place(k)
@@ -215,8 +290,8 @@
         pl.when(k == 2)(lambda: weights(1, wait))
         pl.when(k == 12)(lambda: weights(3, wait))
 
-        x_load(k).wait()
-        pl.when(k + 1 < last)(lambda: x_load(k + 1).start())
+        pl.when(from_rows(k))(lambda: x_load(k).wait())
+        pl.when(jnp.logical_and(from_rows(k), k + 1 < last))(lambda: x_load(k + 1).start())
 
         step = 16 if capacity % 16 == 0 else capacity
         def norm(r, c):
@@ -255,6 +330,8 @@
         token_copy(mine(c), j, c, hs_s, hs_r, sib).start()
         token_copy(mine(c), j, c, hy_s, hy_r, across).start()
     own_start(0, group)
+    squares[...] = jnp.zeros_like(squares)
+    logits[...] = jnp.zeros_like(logits)
 
     def round_(r, c):
         @pl.when(r == 1)
@@ -262,17 +339,13 @@
             for c in range(CHUNKS):
                 token_copy(mine(c), sib, c, hs_s, hs_r, sib).wait_recv()
 
-        @pl.when(r == 4)
-        def _():
-            forward(6, CHUNKS)
-            arrivals(group, 4, 5)
-
         @pl.when(r == 5)
         def _():
             for c in range(CHUNKS):
                 token_copy(mine(c), sib, c, hf_s, hf_r, sib).wait_recv()
 
-        pick_rows(r)
+        pl.when(r == 4)(pick_first_across)
+        pl.when(r != 4)(lambda: pick_rows(r))
         pl.when(r == 1)(lambda: arrivals(0, 0, 2))
         pl.when(r == 2)(lambda: arrivals(0, 2, 4))
 
@@ -296,7 +369,7 @@
         def upto(r):
             return (jnp.where(r >= 3, 4, 0) + jnp.where(r >= 4, 2, 0) + jnp.where(r >= 5, 2, 0) + jnp.where(r >= 7, 8, 0))
         lo, hi = upto(r - 1), upto(r)
-        pl.when(lo < hi)(lambda: x_load(lo).start())
+        pl.when(jnp.logical_and(lo < hi, r != 4))(lambda: x_load(lo).start())
         lax.fori_loop(lo, hi, lambda k, last: block(k, last), hi)
         return c
 
@@ -326,7 +399,7 @@
     lax.fori_loop(0, blocks, arrived, 0)
 
 
-def run_moe(hidden, positions, gain, w_gate, w_up, w_down, capacity):
+def run_moe(hidden, positions, gain, router, w_gate, w_up, w_down, capacity):
     tokens, d_model = hidden.shape
     experts, ff, width = w_gate.shape
     bf16, f32, dma = jnp.bfloat16, jnp.float32, pltpu.SemaphoreType.DMA
@@ -337,11 +410,12 @@
         (3, experts, ff, d_model),
         (E, experts * capacity, d_model),
     )
-    return pl.pallas_call(
+    logits = jax.ShapeDtypeStruct((tokens, router.shape[0]), f32)
+    results = pl.pallas_call(
         moe_kernel,
-        out_shape=tuple(jax.ShapeDtypeStruct(shape, bf16) for shape in shapes),
-        in_specs=[HBM, VMEM, VMEM] + [HBM] * 3,
-        out_specs=(HBM,) * 4,
+        out_shape=tuple(jax.ShapeDtypeStruct(shape, bf16) for shape in shapes) + (logits,),
+        in_specs=[HBM, VMEM, VMEM, VMEM] + [HBM] * 3,
+        out_specs=(HBM,) * 4 + (VMEM,),
         scratch_shapes=[
             pltpu.VMEM((2, 3, ff, d_model), bf16),
             pltpu.VMEM((2, capacity, d_model), bf16),
@@ -352,12 +426,14 @@
             pltpu.VMEM((2 * capacity, tokens), bf16),
             pltpu.VMEM((2, tokens, d_model // COLS), bf16),
             pltpu.VMEM((2, 2 * capacity, d_model // COLS), bf16),
+            pltpu.VMEM((tokens, 1), f32),
         ] + [dma((CHUNKS,)) for _ in range(6)] + [dma((pieces, F)) for _ in range(5)] + [
-            dma((2, 3 * F)), dma((2,)), dma((O_SLOTS,)), dma((E * experts,)), dma((2,)), dma((2,)),
+            dma((2, 3 * F)), dma((2,)), dma((O_SLOTS,)), dma((E * experts,)), dma((2,)), dma((2,)), dma((COLS,)),
         ],
         compiler_params=pltpu.CompilerParams(has_side_effects=True, vmem_limit_bytes=63 * 1024 * 1024),
         name='moe',
-    )(hidden, positions, gain, w_gate, w_up, w_down)[0]
+    )(hidden, positions, gain, router, w_gate, w_up, w_down)
+    return results[0], results[-1]
 
 
 TILE = 128
@@ -365,7 +441,7 @@
 WINDOWS = 32
 
 
-def combine_kernel(starts, slots, probs, hid, back, out, buf, base, count, acc, sem):
+def combine_kernel(starts, lists, logits, hid, back, out, buf, base, count, acc, sem):
     i = pl.program_id(0)
     num_experts = starts.shape[0] // (pl.num_programs(0) + 1)
     capacity = back.shape[0] // num_experts
@@ -397,6 +473,15 @@
             return lax.fori_loop(lo // SPAN, jnp.where(hi > lo, (hi + SPAN - 1) // SPAN, lo // SPAN), one, n)
         count[s] = lax.fori_loop(0, num_experts, expert, jnp.int32(0))
 
+    by_token = lists[...].T
+    slots = [by_token[:, k:k + 1] for k in range(2)]
+    expert_ids = lax.broadcasted_iota(jnp.int32, logits.shape, 1)
+    r0, r1 = [
+        jnp.sum(jnp.where(by_token[:, 2 + k:3 + k] == expert_ids, logits[...], 0.0), axis=1, keepdims=True) for k in range(2)]
+    top = jnp.maximum(r0, r1)
+    e0, e1 = jnp.exp(r0 - top), jnp.exp(r1 - top)
+    p0, p1 = e0 / (e0 + e1), e1 / (e0 + e1)
+
     def use(turn, s):
         def arrived(n, c):
             window(0, s, 0).wait()
@@ -407,8 +492,7 @@
         for n in range(WINDOWS):
             row = jnp.where(lane // SPAN == n, base[s, n], row)
         row = row + lane % SPAN
-        pick = jnp.where(slots[0] == row, 1.0, 0.0).astype(jnp.bfloat16)
-        p0, p1 = probs[0, :TILE], probs[0, TILE:]
+        pick = jnp.concatenate([jnp.where(slot == row, 1.0, 0.0) for slot in slots], axis=0).astype(jnp.bfloat16)
 
         def column(n, c):
             ns = pl.ds(pl.multiple_of(n * cols, 128), cols)
@@ -435,19 +519,22 @@
     out[...] = acc[...].astype(out.dtype)
 
 
-def combine(hidden, back, starts, slots, probs):
+def combine(hidden, back, starts, lists, logits):
     tokens, d_model = hidden.shape
     tiles = tokens // TILE
-    column = pl.BlockSpec((1, 2 * TILE, 1), lambda i: (i, 0, 0))
     row = pl.BlockSpec((TILE, d_model), lambda i: (i, 0))
 
-    def by_tile(x):
-        return jnp.swapaxes(x.reshape(2, tiles, TILE), 0, 1).reshape(tiles, 2 * TILE, 1)
     return pl.pallas_call(
         combine_kernel,
         grid=(tiles,),
         out_shape=jax.ShapeDtypeStruct(hidden.shape, hidden.dtype),
-        in_specs=[pl.BlockSpec(memory_space=pltpu.SMEM), column, column, row, HBM],
+        in_specs=[
+            pl.BlockSpec(memory_space=pltpu.SMEM),
+            pl.BlockSpec((lists.shape[0], TILE), lambda i: (0, i)),
+            pl.BlockSpec((TILE, logits.shape[1]), lambda i: (i, 0)),
+            row,
+            HBM,
+        ],
         out_specs=row,
         scratch_shapes=[
             pltpu.VMEM((2, WINDOWS * SPAN, d_model), jnp.bfloat16),
@@ -458,16 +545,7 @@
         ],
         compiler_params=pltpu.CompilerParams(dimension_semantics=('arbitrary',)),
         name='combine',
-    )(starts.reshape(-1), by_tile(slots), by_tile(probs), hidden, back)
-
-
-def gate_values(hidden_f32, norm_gain, w_router, top2_ids):
-    mean_sq = jnp.mean(hidden_f32 * hidden_f32, axis=-1, keepdims=True)
-    normed = (hidden_f32 * lax.rsqrt(mean_sq + EPS) * norm_gain.astype(jnp.float32)).astype(jnp.bfloat16)
-    logits = jnp.dot(normed, w_router, preferred_element_type=jnp.float32)
-    experts = jnp.arange(w_router.shape[1], dtype=jnp.int32)
-    picked = [jnp.sum(jnp.where(top2_ids[:, k:k + 1] == experts, logits, 0.0), axis=1) for k in range(2)]
-    return jax.nn.softmax(jnp.stack(picked, axis=1), axis=-1)
+    )(starts.reshape(-1), lists, logits, hidden, back)
 
 
 def local_block(hidden, norm_gain, w_router, w_gate, w_up, w_down, top2_ids):
@@ -486,14 +564,14 @@
     positions = positions.reshape(E * experts, 1, tok_local)
 
     gain = norm_gain.astype(jnp.float32).reshape(1, d_model)
-    back = run_moe(hidden, positions, gain, jnp.swapaxes(w_gate, 1, 2), jnp.swapaxes(w_up, 1, 2), w_down, capacity)
+    back, logits = run_moe(hidden, positions, gain, w_router.T, jnp.swapaxes(w_gate, 1, 2), jnp.swapaxes(w_up, 1, 2), w_down, capacity)
     back = back.reshape(num_experts * capacity, d_model)
 
-    gate_probs = gate_values(hidden.astype(jnp.float32), norm_gain, w_router, top2_ids)
-    slots = jnp.stack([jnp.where(place[k] < capacity, top2_ids[:, k] * capacity + place[k], -1) for k in range(2)])
+    rows = [jnp.where(place[k] < capacity, top2_ids[:, k] * capacity + place[k], -1) for k in range(2)]
+    lists = jnp.stack(rows + [top2_ids[:, 0], top2_ids[:, 1]] + [jnp.zeros_like(place[0])] * 4)
     counts = jnp.minimum(before[:, TILE - 1::TILE].T + 1, capacity)
     starts = jnp.concatenate([jnp.zeros((1, num_experts), jnp.int32), counts], axis=0)
-    return combine(hidden, back, starts, slots, gate_probs.T)
+    return combine(hidden, back, starts, lists, logits)
 
 
 def solution(mesh):

time: 977 us -> 963 us (0.986)
  transfers between devices with their start and end apart: 1 -> 1, of which waited for: 0 -> 0; matrix products, arithmetic and copies ran while one was open for 2% -> 0% of each run, Pallas kernels for 0% -> 0%
where the time goes in v4:
time: 963 us; the launch traced here: 949 us
  Pallas kernels  933 us (97%)
    pallas_call x1, Pallas kernels, run_moe(): pl.pallas_call(moe_kernel, out_shape=tuple((jax.ShapeDtypeStruct(shape, b...  869 us
    pallas_call x1, Pallas kernels, combine(): pl.pallas_call(combine_kernel, grid=(tiles,), out_shape=jax.ShapeDtypeStr...  64.5 us
  transfers between devices with their start and end apart: 1, of which 0 were waited for; matrix products, arithmetic and copies ran while one was open for 0% of the time, Pallas kernels for 0%

profile of v4, /device:TPU:1, one launch (start us, length us, event | category | flops | bytes accessed | tf_op | source)
XLA Modules:
  0.0 949.2 jit_solution(11356277775459481976)
XLA Ops:
  0.0 0.8 slice_bitcast_fusion
  0.9 4.5 reduce-window.6
  5.4 0.4 slice_reduce_fusion
  5.8 0.2 reduce-window.9
  6.0 0.1 select_reduce_fusion
  6.2 0.8 or_select_fusion
  6.9 4.3 all-to-all-start
  11.2 0.3 copy.9
  11.6 0.8 compare_select_fusion
  12.4 1.3 reshape.164
  13.7 0.7 reshape.159.starts
  14.4 0.7 stack.9.lists
  15.1 0.0 all-to-all-done
  15.1 0.8 reshape.160.pos
  15.9 868.7 %moe.1 = (bf16[16,320,4096]{2,1,0:T(8,128)(2,1)}, bf16[4,2048,4096]{2,1,0:T(8,128)(2,1)}, bf16[3,4,688,4096]{3,2,1,0:T(8,128)(2,1)}, bf16[4,1280,4096]{2,1,0:T(8,128)(2,1)}, f32[2048,16]{1,0:T(8,128)}) custom-call(bf16[2048,4096]{1,0:T(8,128)(2,1)} %hid.3, s32[16,1,2048]{2,1,0:T(1,128)} %reshape.160.pos, f32[1,4096]{1,0:T(1,128)} %bitcast.32, ...), custom_call_target="tpu_custom_call" | custom-call | tf_op jit(solution)/shard_map/moe/pallas_call | solution.py:414
  884.6 64.5 %combine.1 = bf16[2048,4096]{1,0:T(8,128)(2,1)} custom-call(s32[272]{0:T(512)} %reshape.159.starts, s32[8,2048]{1,0:T(8,128)} %stack.9.lists, f32[2048,16]{1,0:T(8,128)} %get-tuple-element.7.logits, bf16[2048,4096]{1,0:T(8,128)(2,1)} %hid.3, bf16[5120,4096]{1,0:T(8,128)(2,1)} %bitcast.21), custom_call_target="tpu_custom_call" | custom-call | tf_op jit(solution)/shard_map/combine/pallas_call | solution.py:527
  (7 shorter events, 0.1 us)
Async XLA Ops:
  6.9 8.2 all-to-all-start

commit v5 on v4

--- a/solution.py
+++ b/solution.py
@@ -281,11 +281,16 @@
 
         @pl.when(k == 8)
         def _():
-            arrivals(group, 13, steps)
-            swapped(group, 2 * group)
+            arrivals(group, 13, steps - 3)
+            swapped(group, group + 3)
             weights(2, start)
+            weights(2, wait)
+        pl.when(k == 9)(lambda: arrivals(group, steps - 3, steps))
+
+        @pl.when(k == 10)
+        def _():
+            swapped(group + 3, 2 * group)
             weights(3, start)
-            weights(2, wait)
         pl.when(k == 0)(lambda: weights(0, wait))
         pl.when(k == 2)(lambda: weights(1, wait))
         pl.when(k == 12)(lambda: weights(3, wait))
@@ -346,7 +351,8 @@
 
         pl.when(r == 4)(pick_first_across)
         pl.when(r != 4)(lambda: pick_rows(r))
-        pl.when(r == 1)(lambda: arrivals(0, 0, 2))
+        pl.when(r == 0)(lambda: arrivals(0, 0, 1))
+        pl.when(r == 1)(lambda: arrivals(0, 1, 2))
         pl.when(r == 2)(lambda: arrivals(0, 2, 4))
 
         @pl.when(r == 3)
@@ -438,7 +444,7 @@
 
 TILE = 128
 SPAN = 16
-WINDOWS = 32
+WINDOWS = 40
 
 
 def combine_kernel(starts, lists, logits, hid, back, out, buf, base, count, acc, sem):

time: 963 us -> 957 us (level); the launches traced: 949 us -> 955 us
  no operation moved by 1% of the time
where the time goes in v5:
time: 957 us; the launch traced here: 955 us
  Pallas kernels  939 us (98%)
    pallas_call x1, Pallas kernels, run_moe(): pl.pallas_call(moe_kernel, out_shape=tuple((jax.ShapeDtypeStruct(shape, b...  869 us
    pallas_call x1, Pallas kernels, combine(): pl.pallas_call(combine_kernel, grid=(tiles,), out_shape=jax.ShapeDtypeStr...  70.1 us
  transfers between devices with their start and end apart: 1, of which 0 were waited for; matrix products, arithmetic and copies ran while one was open for 0% of the time, Pallas kernels for 0%

profile of v5, /device:TPU:1, one launch (start us, length us, event | category | flops | bytes accessed | tf_op | source)
XLA Modules:
  0.0 954.7 jit_solution(413209319782552559)
XLA Ops:
  0.0 0.8 slice_bitcast_fusion
  0.9 4.5 reduce-window.6
  5.4 0.4 slice_reduce_fusion
  5.8 0.2 reduce-window.9
  6.0 0.1 select_reduce_fusion
  6.2 0.8 or_select_fusion
  6.9 4.3 all-to-all-start
  11.2 0.3 copy.9
  11.6 0.8 compare_select_fusion
  12.4 1.3 reshape.164
  13.7 0.7 reshape.159.starts
  14.4 0.7 stack.9.lists
  15.1 0.0 all-to-all-done
  15.1 0.8 reshape.160.pos
  15.9 868.7 %moe.1 = (bf16[16,320,4096]{2,1,0:T(8,128)(2,1)}, bf16[4,2048,4096]{2,1,0:T(8,128)(2,1)}, bf16[3,4,688,4096]{3,2,1,0:T(8,128)(2,1)}, bf16[4,1280,4096]{2,1,0:T(8,128)(2,1)}, f32[2048,16]{1,0:T(8,128)}) custom-call(bf16[2048,4096]{1,0:T(8,128)(2,1)} %hid.3, s32[16,1,2048]{2,1,0:T(1,128)} %reshape.160.pos, f32[1,4096]{1,0:T(1,128)} %bitcast.32, ...), custom_call_target="tpu_custom_call" | custom-call | tf_op jit(solution)/shard_map/moe/pallas_call | solution.py:420
  884.6 70.1 %combine.1 = bf16[2048,4096]{1,0:T(8,128)(2,1)} custom-call(s32[272]{0:T(512)} %reshape.159.starts, s32[8,2048]{1,0:T(8,128)} %stack.9.lists, f32[2048,16]{1,0:T(8,128)} %get-tuple-element.7.logits, bf16[2048,4096]{1,0:T(8,128)(2,1)} %hid.3, bf16[5120,4096]{1,0:T(8,128)(2,1)} %bitcast.21), custom_call_target="tpu_custom_call" | custom-call | tf_op jit(solution)/shard_map/combine/pallas_call | solution.py:533
  (7 shorter events, 0.1 us)
Async XLA Ops:
  6.9 8.2 all-to-all-start
